TPU v7x, 8 devices: a whole 2x2x1 slice. The times are simulated.
8 devices in a mesh: dp: 1 (over z), ep: 8 (over y, x, core).
Axes of the slice: x: 2, y: 2, z: 1, core: 2. Of those that a mesh axis runs over, the one named last changes fastest.
Arguments:
- hidden: bfloat16 [4096, 2560], P(('dp', 'ep'))
- w_router: bfloat16 [2560, 64], replicated
- w_gate: bfloat16 [64, 2560, 1536], P('ep')
- w_up: bfloat16 [64, 2560, 1536], P('ep')
- w_down: bfloat16 [64, 1536, 2560], P('ep')
- shared_gate: bfloat16 [2560, 3072], replicated
- shared_up: bfloat16 [2560, 3072], replicated
- shared_down: bfloat16 [3072, 2560], replicated
- top_idx: int32 [4096, 6], P(('dp', 'ep'))
- keep_mask: int32 [4096, 6], P(('dp', 'ep'))
Outputs:
- output: bfloat16 [4096, 2560], P(('dp', 'ep'))
All inputs are finite; a program needn't handle non-finite values.
Results may differ from a plain program's by a relative error of at most 0.00691395.
Values are sent between devices in bfloat16 or wider.
A program may use at most 1 GiB of HBM per device.

v0:
```python
import jax
import jax.numpy as jnp
from jax import lax
from jax.sharding import PartitionSpec as P

ROUTE_SCALE = 16.0


def swiglu(tok_rows, gate_w, up_w, down_w):
    h_gate = jnp.dot(tok_rows, gate_w, preferred_element_type=jnp.float32)
    h_up = jnp.dot(tok_rows, up_w, preferred_element_type=jnp.float32)
    act_rows = (jax.nn.silu(h_gate) * h_up).astype(jnp.bfloat16)
    return jnp.dot(act_rows, down_w, preferred_element_type=jnp.float32)


def expert_bank(tok_rows, gate_w, up_w, down_w):
    h_gate = jnp.einsum("erd,edf->erf", tok_rows, gate_w, preferred_element_type=jnp.float32)
    h_up = jnp.einsum("erd,edf->erf", tok_rows, up_w, preferred_element_type=jnp.float32)
    act_rows = (jax.nn.silu(h_gate) * h_up).astype(jnp.bfloat16)
    return jnp.einsum("erf,efd->erd", act_rows, down_w, preferred_element_type=jnp.float32)


def route_gates(hidden, w_router, top_idx, keep_mask):
    logits = jnp.dot(hidden, w_router, preferred_element_type=jnp.float32)
    router_prob = jax.nn.softmax(logits, axis=-1)
    return ROUTE_SCALE * jnp.take_along_axis(router_prob, top_idx, axis=1) * keep_mask.astype(jnp.float32)


def solution(mesh):
    groups = mesh.shape["ep"]
    tok_spec = P(("dp", "ep"), None)
    bank_spec = P("ep", None, None)

    def device_fn(hidden, w_router, w_gate, w_up, w_down, shared_gate, shared_up, shared_down, top_idx, keep_mask):
        tokens, top_k = top_idx.shape
        hidden_dim = hidden.shape[1]
        experts = w_router.shape[1]
        per_dev = w_gate.shape[0]
        capacity = 8 * ((top_k * tokens + 4 * experts - 1) // (4 * experts))
        n_rows = experts * capacity
        gate_vals = route_gates(hidden, w_router, top_idx, keep_mask)
        pair_expert = top_idx.reshape(-1)
        pair_kept = keep_mask.reshape(-1) > 0
        onehot = ((pair_expert[:, None] == jnp.arange(experts)[None, :]) & pair_kept[:, None]).astype(jnp.int32)
        pair_slot = jnp.sum((jnp.cumsum(onehot, axis=0) - 1) * onehot, axis=1)
        dest_dev = pair_expert // per_dev
        local_exp = pair_expert % per_dev
        dest_row = jnp.where(pair_kept, (local_exp * groups + dest_dev) * capacity + pair_slot, n_rows)
        pair_token = jnp.arange(tokens * top_k, dtype=jnp.int32) // top_k
        row_token = jnp.full((n_rows,), tokens, jnp.int32).at[dest_row].set(pair_token, mode="drop")
        send_rows = jnp.take(hidden, row_token, axis=0, mode="fill", fill_value=0).reshape(per_dev, groups, capacity, hidden_dim)
        recv_rows = lax.all_to_all(send_rows, "ep", 1, 1, tiled=True)
        expert_out = expert_bank(recv_rows.reshape(per_dev, groups * capacity, hidden_dim), w_gate, w_up, w_down).astype(jnp.bfloat16)
        back_rows = lax.all_to_all(expert_out.reshape(per_dev, groups, capacity, hidden_dim), "ep", 1, 1, tiled=True)
        picked = jnp.take(back_rows.reshape(n_rows, hidden_dim), dest_row, axis=0, mode="fill", fill_value=0).reshape(tokens, top_k, hidden_dim)
        routed = jnp.sum(gate_vals[:, :, None] * picked.astype(jnp.float32), axis=1)
        shared = swiglu(hidden, shared_gate, shared_up, shared_down)
        return (shared + routed).astype(jnp.bfloat16)

    return jax.shard_map(device_fn, mesh=mesh, in_specs=(tok_spec, P(), bank_spec, bank_spec, bank_spec, P(), P(), P(), tok_spec, tok_spec), out_specs=tok_spec, check_vma=False)
```

profile of v0, /device:TPU:0, one launch (start us, length us, event | category | flops | bytes accessed | tf_op | source)
XLA Modules:
  0.0 1254.1 jit_solution(7654280666346763386)
XLA Ops:
  0.0 1.0 copy.70
  1.0 0.2 eq.28
  1.2 0.2 reshape.223
  1.4 0.7 broadcast_compare_fusion
  2.1 0.2 copy.71
  2.3 0.2 gt.28
  2.5 0.2 gt.27
  2.7 0.2 reshape.225
  2.9 0.2 gt.29
  3.1 1.0 fusion.8
  4.1 31.9 %reduce-window.6 = s32[64,24,128]{2,1,0:T(8,128)S(1)} reduce-window(s32[64,24,128]{2,1,0:T(8,128)} %fusion.8, s32[]{:T(128)} %constant.87.clone.1), window={size=1x1x128 pad=0_0x0_0x127_0}, to_apply=%region_2.0 | reduce-window | flops 24969216 | bytes 1572868 | tf_op jit(solution)/shard_map/reduce-window
  36.0 1.2 slice.14
  37.1 1.6 copy.85
  38.7 0.2 reduce-window.9
  38.9 0.3 add_add_fusion
  39.2 0.2 fusion.5
  39.4 0.1 compare_select_fusion
  39.5 0.5 copy-done.5
  40.0 11.8 scatter_custom_fusion
  51.9 0.1 broadcast_in_dim.48
  52.0 32.6 %gather_fusion = bf16[6144,2560]{1,0:T(8,128)(2,1)} fusion(bf16[512,2560]{1,0:T(8,128)(2,1)S(1)} %copy-done, s32[6144]{0:T(1024)S(1)} %fusion.11), kind=kCustom, calls=%fused_computation | custom fusion | bytes 62939136 | tf_op jit(solution)/shard_map/jit(_take)/gather | solution.py:51
  84.5 21.6 %copy_select_fusion = bf16[8,8,96,2560]{3,2,0,1:T(8,128)(2,1)} fusion(bf16[8,8,96,2560]{3,2,1,0:T(8,128)(2,1)} %bitcast.47, pred[8,8,96]{2,0,1:T(8,128)(4,1)S(1)} %copy.80), kind=kLoop, calls=%fused_computation.6 | loop fusion | flops 15728640 | bytes 62920704 | tf_op jit(solution)/shard_map/jit(_take)/select_n | solution.py:51
  106.2 351.6 %all_to_all.10 = bf16[8,8,96,2560]{3,2,0,1:T(8,128)(2,1)} all-to-all(bf16[8,8,96,2560]{3,2,0,1:T(8,128)(2,1)} %copy_select_fusion), channel_id=1, replica_groups=mesh['dp'=1,'ep'=8] {'ep'}, dimensions={1} | all-to-all | bytes 62914560 | tf_op jit(solution)/shard_map/all_to_all | solution.py:52
  457.8 21.7 %copy.82 = bf16[8,8,96,2560]{3,2,1,0:T(8,128)(2,1)} copy(bf16[8,8,96,2560]{3,2,0,1:T(8,128)(2,1)} %all_to_all.10) | data formatting | bytes 62914560 | tf_op jit(solution)/shard_map/all_to_all | solution.py:52
  479.5 60.4 %fusion.32 = f32[8,768,1536]{2,1,0:T(8,128)} fusion(bf16[8,768,2560]{2,1,0:T(8,128)(2,1)} %bitcast.48, bf16[8,2560,1536]{2,1,0:T(8,128)(2,1)} %param.12), kind=kOutput, calls=%fused_computation.71 | convolution fusion | flops 48318382080 | bytes 132120576 | tf_op jit(solution)/shard_map/erd,edf->erf/dot_general | solution.py:17
  539.9 64.8 %multiply_convert_fusion.clone.6 = bf16[8,768,1536]{2,1,0:T(8,128)(2,1)} fusion(f32[8,768,1536]{2,1,0:T(8,128)} %fusion.32, bf16[8,768,2560]{2,1,0:T(8,128)(2,1)} %bitcast.49, bf16[8,2560,1536]{2,1,0:T(8,128)(2,1)} %param.13), kind=kOutput, calls=%fused_computation.5.clone.clone.clone.clone.clone.1 | convolution fusion | flops 48375005184 | bytes 150994944 | tf_op jit(solution)/shard_map/erd,edf->erf/dot_general | solution.py:18
  604.7 67.8 %fusion.1 = bf16[8,768,2560]{2,1,0:T(8,128)(2,1)} fusion(bf16[8,1536,2560]{2,1,0:T(8,128)(2,1)} %param.14, bf16[8,768,1536]{2,1,0:T(8,128)(2,1)} %multiply_convert_fusion.clone.6), kind=kOutput, calls=%fused_computation.8 | convolution fusion | flops 48334110720 | bytes 113246208 | tf_op jit(solution)/shard_map/erf,efd->erd/dot_general | solution.py:20
  672.5 21.7 %copy.83 = bf16[8,8,96,2560]{3,2,0,1:T(8,128)(2,1)} copy(bf16[8,8,96,2560]{3,2,1,0:T(8,128)(2,1)} %bitcast.50) | data formatting | bytes 62914560 | tf_op jit(solution)/shard_map/reshape | solution.py:54
  694.1 0.0 copy-start.4
  694.2 0.0 copy-start.1
  694.2 6.1 all-to-all-start.1
  700.3 0.2 reduce_sum.33
  700.5 0.1 copy.76
  700.6 0.8 copy.77
  701.5 0.1 copy.67
  701.6 0.2 reshape.245
  701.8 0.9 fusion.30
  702.8 24.9 %gather_fusion.2 = f32[3072]{0:T(1024)S(1)} fusion(f32[512,64]{0,1:T(8,128)S(1)} %fusion.9, s32[3072]{0:T(1024)S(1)} %reshape.245), kind=kCustom, calls=%fused_computation.2 | custom fusion | bytes 49152 | tf_op jit(solution)/shard_map/jit(take_along_axis)/gather | solution.py:26
  727.7 0.2 reshape.248
  728.0 0.1 copy.68
  728.1 0.1 copy.69
  728.3 13.4 %fusion.31 = f32[512,3072]{1,0:T(8,128)} fusion(bf16[512,2560]{1,0:T(8,128)(2,1)S(1)} %copy-done, bf16[2560,3072]{1,0:T(8,128)(2,1)} %param.15), kind=kOutput, calls=%fused_computation.70 | convolution fusion | flops 8053063680 | bytes 24641536 | tf_op jit(solution)/shard_map/dot_general | solution.py:10
  741.7 300.0 %all-to-all-done.1 = bf16[8,8,96,2560]{3,2,0,1:T(8,128)(2,1)} async-done(((bf16[8,8,96,2560]{3,2,0,1:T(8,128)(2,1)}), bf16[8,8,96,2560]{3,2,0,1:T(8,128)(2,1)}, u32[]{:S(2)}, u32[]{:S(2)}) %all-to-all-start.1) | async-done | bytes 31457312 | tf_op jit(solution)/shard_map/all_to_all | solution.py:54
  1041.7 21.7 %copy.84 = bf16[8,8,96,2560]{3,2,1,0:T(8,128)(2,1)} copy(bf16[8,8,96,2560]{3,2,0,1:T(8,128)(2,1)} %all-to-all-done.1) | data formatting | bytes 62914560 | tf_op jit(solution)/shard_map/all_to_all | solution.py:54
  1063.4 110.0 %gather_fusion.1 = bf16[3072,2560]{1,0:T(8,128)(2,1)} fusion(bf16[6144,2560]{1,0:T(8,128)(2,1)} %bitcast.46, s32[3072]{0:T(1024)S(1)} %broadcast_clamp_fusion), kind=kCustom, calls=%fused_computation.1 | custom fusion | bytes 31469568 | tf_op jit(solution)/shard_map/jit(_take)/gather | solution.py:55
  1173.3 24.9 %gather.20 = bf16[512,6,2560]{2,1,0:T(8,128)(2,1)} reshape(bf16[3072,2560]{1,0:T(8,128)(2,1)} %gather_fusion.1) | data formatting | bytes 31457280 | tf_op jit(solution)/shard_map/jit(_take)/gather | solution.py:55
  1198.2 25.9 %multiply_reduce_fusion = f32[512,2560]{1,0:T(8,128)} fusion(bf16[512,6,2560]{2,1,0:T(8,128)(2,1)} %gather.20, f32[512,6]{1,0:T(8,128)S(1)} %copy.69, pred[512,6]{1,0:T(8,128)(4,1)S(1)} %copy-done.2), kind=kLoop, calls=%fused_computation.4 | loop fusion | flops 30146560 | bytes 20986880 | tf_op jit(solution)/shard_map/reduce_sum | solution.py:56
  1224.1 30.0 %add_convert_fusion = bf16[512,2560]{1,0:T(8,128)(2,1)} fusion(f32[512,2560]{1,0:T(8,128)} %multiply_reduce_fusion, bf16[3072,2560]{1,0:T(8,128)(2,1)} %param.17, f32[512,3072]{1,0:T(8,128)} %fusion.31, bf16[512,2560]{1,0:T(8,128)(2,1)S(1)} %copy-done, bf16[2560,3072]{1,0:T(8,128)(2,1)} %param.16), kind=kOutput, calls=%fused_computation.11 | convolution fusion | flops 16118185984 | bytes 48234496 | tf_op jit(solution)/shard_map/dot_general | solution.py:13
  (25 shorter events, 0.2 us)
Async XLA Ops:
  0.0 52.0 %copy-start = (bf16[512,2560]{1,0:T(8,128)(2,1)S(1)}, bf16[512,2560]{1,0:T(8,128)(2,1)}, u32[]{:S(2)}) copy-start(bf16[512,2560]{1,0:T(8,128)(2,1)} %param.10) | copy-start | bytes 7864324
  39.4 0.6 copy-start.5
  40.0 44.5 %copy-start.7 = (s32[3072,1]{0,1:T(1,128)}, s32[3072,1]{0,1:T(1,128)S(1)}, u32[]{:S(2)}) copy-start(s32[3072,1]{0,1:T(1,128)S(1)} %compare_select_fusion) | copy-start | bytes 36868
  694.1 6.1 copy-start.6
  694.1 6.5 copy-start.3
  694.1 6.5 copy-start.4
  694.2 7.6 copy-start.1
  694.2 347.5 %all-to-all-start.1 = ((bf16[8,8,96,2560]{3,2,0,1:T(8,128)(2,1)}), bf16[8,8,96,2560]{3,2,0,1:T(8,128)(2,1)}, u32[]{:S(2)}, u32[]{:S(2)}) async-start(bf16[8,8,96,2560]{3,2,0,1:T(8,128)(2,1)} %copy.83), calls=%async_computation.1 | async-start | bytes 62914560 | tf_op jit(solution)/shard_map/all_to_all | solution.py:54
  702.8 25.4 %copy-start.8 = (s32[3072,1]{0,1:T(1,128)S(1)}, s32[3072,1]{0,1:T(1,128)}, u32[]{:S(2)}) copy-start(s32[3072,1]{0,1:T(1,128)} %copy-done.7) | copy-start | bytes 36868
  1173.3 24.9 %copy-start.2 = (pred[512,6]{1,0:T(8,128)(4,1)S(1)}, pred[512,6]{1,0:T(8,128)(4,1)}, u32[]{:S(2)}) copy-start(pred[512,6]{1,0:T(8,128)(4,1)} %copy.77) | copy-start | bytes 9220
where the time goes:
time: 1270 us; the launch traced here: 1250 us
  blocking collectives  352 us (28%)
  waiting for transfers between devices  300 us (24%)
  local copies, waits for them, and re-layouts  277 us (22%)
  matrix products  237 us (19%)
  other arithmetic  82.1 us (6%)
    all_to_all x1, blocking collectives, device_fn(): recv_rows = lax.all_to_all(send_rows, 'ep', 1, 1, tiled=True)  352 us
    all_to_all x1, waiting for transfers between devices, device_fn(): lax.all_to_all(expert_out.reshape(per_dev, groups, capacity, hidden_dim),...  300 us
    gather x2, local copies, waits for them, and re-layouts, device_fn(): jnp.take(back_rows.reshape(n_rows, hidden_dim), dest_row, axis=0, mode='f...  135 us
    dot_general x1, matrix products, expert_bank(): jnp.einsum('erf,efd->erd', act_rows, down_w, preferred_element_type=jnp.f...  67.8 us
    dot_general x1, matrix products, expert_bank(): jnp.einsum('erd,edf->erf', tok_rows, up_w, preferred_element_type=jnp.flo...  64.8 us
    dot_general x1, matrix products, expert_bank(): jnp.einsum('erd,edf->erf', tok_rows, gate_w, preferred_element_type=jnp.f...  60.4 us
    gather x1, local copies, waits for them, and re-layouts, device_fn(): jnp.take(hidden, row_token, axis=0, mode='fill', fill_value=0)  32.6 us
    another operation x2, other arithmetic  32.1 us
  transfers between devices with their start and end apart: 1, of which 1 were waited for; matrix products, arithmetic and copies ran while one was open for 3% of the time, Pallas kernels for 0%

commit v1 on v0

v1 whole, which is shorter than its diff:
```python
import functools

import jax
import jax.numpy as jnp
from jax import lax
from jax.experimental import pallas as pl
from jax.experimental.pallas import tpu as pltpu
from jax.sharding import PartitionSpec as P

ROUTE_SCALE = 16.0
CAP = 96
VMEM_BYTES = 66_900_000
MESH = pl.DeviceIdType.MESH
F32 = jnp.float32
BF16 = jnp.bfloat16


def dot(a, b):
    return jnp.dot(a, b, preferred_element_type=F32)


def swiglu(tok_rows, gate_w, up_w, down_w):
    h_gate = dot(tok_rows, gate_w)
    h_up = dot(tok_rows, up_w)
    act_rows = (jax.nn.silu(h_gate) * h_up).astype(BF16)
    return dot(act_rows, down_w)


def route_kernel(x_ref, w_ref, idx_ref, keep_ref, tab_ref):
    experts, tokens = w_ref.shape[1], x_ref.shape[0]
    logits = lax.dot_general(w_ref[...], x_ref[...], (((0,), (1,)), ((), ())), preferred_element_type=F32)
    e = jnp.exp(logits - jnp.max(logits, axis=0, keepdims=True))
    prob = e / jnp.sum(e, axis=0, keepdims=True)
    expert_id = lax.broadcasted_iota(jnp.int32, (experts, tokens), 0)
    member = jnp.zeros((experts, tokens), F32)
    for k in range(idx_ref.shape[0]):
        hit = (expert_id == idx_ref[k : k + 1, :]) & (keep_ref[k : k + 1, :] > 0)
        member = jnp.where(hit, 1.0, member)
    earlier = lax.broadcasted_iota(jnp.int32, (tokens, tokens), 0) < lax.broadcasted_iota(jnp.int32, (tokens, tokens), 1)
    rank = dot(member.astype(BF16), jnp.where(earlier, 1.0, 0.0).astype(BF16))
    slot = jnp.where(member > 0, rank, -1.0)
    gate = ROUTE_SCALE * prob * member
    half = tab_ref.shape[1] // 2
    for d in range(tab_ref.shape[0]):
        tab_ref[d, :half, :] = slot[d * half : (d + 1) * half]
        tab_ref[d, half:, :] = gate[d * half : (d + 1) * half]


def up_kernel(tab_ref, x_hbm, w1_hbm, w3_hbm, act_hbm, xg, xbuf, dbuf, wg, wu, ab, x_sem, w_sem, a_sem):
    groups, tokens, width = x_hbm.shape
    per_dev, _, ff = w1_hbm.shape
    tn = wg.shape[2]
    nt = ff // tn
    steps = per_dev * nt
    xc = 512

    def x_copy(s, slot):
        return pltpu.make_async_copy(x_hbm.at[s], xbuf.at[slot], x_sem.at[slot])

    def w_copies(it, slot):
        e, n = it // nt, lax.rem(it, nt)
        cols = pl.ds(pl.multiple_of(n * tn, tn), tn)
        return (
            pltpu.make_async_copy(w1_hbm.at[e, :, cols], wg.at[slot], w_sem.at[0, slot]),
            pltpu.make_async_copy(w3_hbm.at[e, :, cols], wu.at[slot], w_sem.at[1, slot]),
        )

    def a_copy(it, slot):
        e, n = it // nt, lax.rem(it, nt)
        cols = pl.ds(pl.multiple_of(n * tn, tn), tn)
        return pltpu.make_async_copy(ab.at[slot], act_hbm.at[e, :, cols], a_sem.at[slot])

    x_copy(0, 0).start()
    for c in w_copies(0, 0):
        c.start()
    row = lax.broadcasted_iota(jnp.int32, (CAP, tokens), 0).astype(F32)

    def gather(s, _):
        slot = lax.rem(s, 2)

        @pl.when(s + 1 < groups)
        def _():
            x_copy(s + 1, 1 - slot).start()

        for e in range(per_dev):
            dbuf[e * CAP : (e + 1) * CAP, :] = jnp.where(row == tab_ref[s, e : e + 1, :], 1.0, 0.0).astype(BF16)
        x_copy(s, slot).wait()
        rows = pl.ds(pl.multiple_of(s * CAP, CAP), CAP)

        def cols_step(n, _):
            cols = pl.ds(pl.multiple_of(n * xc, xc), xc)
            got = dot(dbuf[...], xbuf[slot, :, cols]).astype(BF16)
            xg[:, rows, cols] = got.reshape(per_dev, CAP, xc)
            return 0

        lax.fori_loop(0, width // xc, cols_step, 0)
        return 0

    lax.fori_loop(0, groups, gather, 0)

    def main(it, _):
        slot = lax.rem(it, 2)
        e = it // nt

        @pl.when(it + 1 < steps)
        def _():
            for c in w_copies(it + 1, 1 - slot):
                c.start()

        for c in w_copies(it, slot):
            c.wait()

        @pl.when(it >= 2)
        def _():
            a_copy(it - 2, slot).wait()

        h_gate = dot(xg[e], wg[slot])
        h_up = dot(xg[e], wu[slot])
        ab[slot] = (jax.nn.silu(h_gate) * h_up).astype(BF16)
        a_copy(it, slot).start()
        return 0

    lax.fori_loop(0, steps, main, 0)
    a_copy(steps - 2, steps % 2).wait()
    a_copy(steps - 1, (steps - 1) % 2).wait()


def down_kernel(
    tab_ref, act_hbm, w2_hbm, ys_hbm, y_hbm,
    comb, act, part, wbuf, fsend, frecv, mine, bsend, brecv, acc, ybuf,
    act_sem, w_sem, acc_sem, y_sem, fs_sem, fr_sem, bs_sem, br_sem, credit,
):
    groups, pair, tokens = tab_ref.shape
    per_dev = pair // 2
    rows = per_dev * CAP
    cw = wbuf.shape[2]
    nc = acc.shape[0]
    steps = 4 * nc

    me = lax.axis_index("ep")
    core, chip = lax.rem(me, 2), me // 2
    partner = me + 1 - 2 * core
    yb, xb = chip // 2, lax.rem(chip, 2)

    def chip_at(j):
        m = 3 - j
        return 2 * lax.rem(yb + m // 2, 2) + lax.rem(xb + lax.rem(m, 2), 2)

    def w_copy(it, slot):
        c, e = it // per_dev, lax.rem(it, per_dev)
        cols = pl.ds(pl.multiple_of(c * cw, cw), cw)
        return pltpu.make_async_copy(w2_hbm.at[e, :, cols], wbuf.at[slot], w_sem.at[slot])

    def act_copy(e):
        return pltpu.make_async_copy(act_hbm.at[e], act.at[e], act_sem.at[e])

    def acc_copy(c):
        return pltpu.make_async_copy(ys_hbm.at[:, pl.ds(c * cw, cw)], acc.at[c], acc_sem.at[c])

    w_copy(0, 0).start()
    for e in range(per_dev):
        act_copy(e).start()
    for c in range(nc):
        acc_copy(c).start()

    barrier = pltpu.get_barrier_semaphore()
    pl.semaphore_signal(barrier, inc=1, device_id={"ep": partner}, device_id_type=MESH)
    for j in range(3):
        pl.semaphore_signal(barrier, inc=1, device_id={"ep": 2 * chip_at(j) + core}, device_id_type=MESH)
    pl.semaphore_wait(barrier, 4)

    lane = lax.broadcasted_iota(jnp.int32, (per_dev, rows), 1)
    first = lax.broadcasted_iota(jnp.int32, (per_dev, rows), 0) * CAP
    inside = (lane >= first) & (lane < first + CAP)
    spread = jnp.where(inside, 1.0, 0.0).astype(BF16)
    want = jnp.sum(jnp.where(inside, lane - first, 0).astype(F32), axis=0, keepdims=True)

    def over_slots(v):
        return lax.dot_general(v, spread, (((0,), (0,)), ((), ())), preferred_element_type=F32)

    def build(s, _):
        hit = over_slots(tab_ref[s, :per_dev, :].astype(BF16)) == want
        gate = tab_ref[s, per_dev:, :]
        hi = gate.astype(BF16)
        rest = gate - hi.astype(F32)
        mid = rest.astype(BF16)
        low = (rest - mid.astype(F32)).astype(BF16)
        for k, piece in enumerate((hi, mid, low)):
            comb[k, s] = jnp.where(hit, over_slots(piece), 0.0).astype(BF16)
        return 0

    lax.fori_loop(0, groups, build, 0)
    for c in range(nc):
        acc_copy(c).wait()

    def f_copy(slot):
        return pltpu.make_async_remote_copy(
            src_ref=fsend.at[slot], dst_ref=frecv.at[slot], send_sem=fs_sem.at[slot], recv_sem=fr_sem.at[slot],
            device_id={"ep": partner}, device_id_type=MESH)

    def b_copy(j, c):
        slot = lax.rem(c, 2)
        return pltpu.make_async_remote_copy(
            src_ref=bsend.at[j, slot], dst_ref=brecv.at[j, c], send_sem=bs_sem.at[j, slot], recv_sem=br_sem.at[j, c],
            device_id={"ep": 2 * chip_at(j) + core}, device_id_type=MESH)

    def combine(s):
        return dot(comb[0, s], part[s]) + dot(comb[1, s], part[s]) + dot(comb[2, s], part[s])

    def launch(h):
        j = lax.rem(h, 4)

        @pl.when(j < 3)
        def _():
            b_copy(j, h // 4).start()

    def consume(h):
        slot, c, j = lax.rem(h, 2), h // 4, lax.rem(h, 4)
        f_copy(slot).wait_recv()

        @pl.when(j < 3)
        def _():
            @pl.when(c >= 2)
            def _():
                b_copy(j, c - 2).wait_send()

            bsend[j, lax.rem(c, 2)] = (mine[slot] + frecv[slot]).astype(BF16)

        @pl.when(j == 3)
        def _():
            acc[c] = acc[c] + (mine[slot] + frecv[slot])

        @pl.when(h + 2 < steps)
        def _():
            pl.semaphore_signal(credit, inc=1, device_id={"ep": partner}, device_id_type=MESH)

    def chunk(c, _):
        def down(e, _):
            it = c * per_dev + e
            slot = lax.rem(it, 2)

            @pl.when(it + 1 < nc * per_dev)
            def _():
                w_copy(it + 1, 1 - slot).start()

            w_copy(it, slot).wait()

            @pl.when(c == 0)
            def _():
                act_copy(e).wait()

            got = dot(act[e], wbuf[slot]).astype(BF16)
            part[:, pl.ds(pl.multiple_of(e * CAP, CAP), CAP), :] = got.reshape(groups, CAP, cw)
            return 0

        lax.fori_loop(0, per_dev, down, 0)

        def pair_step(j, _):
            g = 4 * c + j
            slot = lax.rem(g, 2)
            q = chip_at(j)

            @pl.when(g >= 2)
            def _():
                f_copy(slot).wait_send()

            fsend[slot] = combine(2 * q + 1 - core)
            mine[slot] = combine(2 * q + core)

            @pl.when(g >= 2)
            def _():
                pl.semaphore_wait(credit, 1)

            f_copy(slot).start()

            @pl.when(g >= 2)
            def _():
                launch(g - 2)

            @pl.when(g >= 1)
            def _():
                consume(g - 1)

            return 0

        lax.fori_loop(0, 4, pair_step, 0)
        return 0

    lax.fori_loop(0, nc, chunk, 0)
    launch(steps - 2)
    consume(steps - 1)
    f_copy(0).wait_send()
    f_copy(1).wait_send()

    def y_copy(c):
        return pltpu.make_async_copy(ybuf.at[c % 2], y_hbm.at[:, pl.ds(c * cw, cw)], y_sem.at[c % 2])

    for c in range(nc):
        for j in range(3):
            b_copy(j, c).wait_recv()
            if c >= nc - 2:
                b_copy(j, c).wait_send()
        if c >= 2:
            y_copy(c - 2).wait()
        total = acc[c]
        for j in range(3):
            total = total + brecv[j, c].astype(F32)
        ybuf[c % 2] = total.astype(BF16)
        y_copy(c).start()
    y_copy(nc - 2).wait()
    y_copy(nc - 1).wait()


def solution(mesh):
    groups = mesh.shape["ep"]
    tok_spec = P(("dp", "ep"), None)
    bank_spec = P("ep", None, None)
    vmem = pl.BlockSpec(memory_space=pltpu.VMEM)
    hbm = pl.BlockSpec(memory_space=pl.ANY)

    def device_fn(hidden, w_router, w_gate, w_up, w_down, shared_gate, shared_up, shared_down, top_idx, keep_mask):
        tokens, width = hidden.shape
        per_dev, _, ff = w_gate.shape
        rows = groups * CAP
        tn, cw = 256, 256
        nc = width // cw
        x_all = lax.all_gather(hidden, "ep", axis=0, tiled=False)
        tab = pl.pallas_call(
            route_kernel,
            out_shape=jax.ShapeDtypeStruct((groups, 2 * per_dev, tokens), F32),
            in_specs=[vmem] * 4,
            out_specs=vmem,
            name="route",
        )(hidden, w_router, top_idx.T, keep_mask.T)
        tab = lax.all_to_all(tab, "ep", 0, 0, tiled=True)
        shared = swiglu(hidden, shared_gate, shared_up, shared_down)
        act = pl.pallas_call(
            up_kernel,
            out_shape=jax.ShapeDtypeStruct((per_dev, rows, ff), BF16),
            in_specs=[vmem, hbm, hbm, hbm],
            out_specs=hbm,
            scratch_shapes=[
                pltpu.VMEM((per_dev, rows, width), BF16),
                pltpu.VMEM((2, tokens, width), BF16),
                pltpu.VMEM((per_dev * CAP, tokens), BF16),
                pltpu.VMEM((2, width, tn), BF16),
                pltpu.VMEM((2, width, tn), BF16),
                pltpu.VMEM((2, rows, tn), BF16),
                pltpu.SemaphoreType.DMA((2,)),
                pltpu.SemaphoreType.DMA((2, 2)),
                pltpu.SemaphoreType.DMA((2,)),
            ],
            compiler_params=pltpu.CompilerParams(vmem_limit_bytes=VMEM_BYTES),
            cost_estimate=pl.CostEstimate(flops=4 * per_dev * rows * width * ff, bytes_accessed=4 * per_dev * width * ff, transcendentals=0),
            name="up",
        )(tab, x_all, w_gate, w_up)
        return pl.pallas_call(
            down_kernel,
            out_shape=jax.ShapeDtypeStruct((tokens, width), BF16),
            in_specs=[vmem, hbm, hbm, hbm],
            out_specs=hbm,
            scratch_shapes=[
                pltpu.VMEM((3, groups, tokens, per_dev * CAP), BF16),
                pltpu.VMEM((per_dev, rows, ff), BF16),
                pltpu.VMEM((groups, per_dev * CAP, cw), BF16),
                pltpu.VMEM((2, ff, cw), BF16),
                pltpu.VMEM((2, tokens, cw), F32),
                pltpu.VMEM((2, tokens, cw), F32),
                pltpu.VMEM((2, tokens, cw), F32),
                pltpu.VMEM((3, 2, tokens, cw), BF16),
                pltpu.VMEM((3, nc, tokens, cw), BF16),
                pltpu.VMEM((nc, tokens, cw), F32),
                pltpu.VMEM((2, tokens, cw), BF16),
                pltpu.SemaphoreType.DMA((per_dev,)),
                pltpu.SemaphoreType.DMA((2,)),
                pltpu.SemaphoreType.DMA((nc,)),
                pltpu.SemaphoreType.DMA((2,)),
                pltpu.SemaphoreType.DMA((2,)),
                pltpu.SemaphoreType.DMA((2,)),
                pltpu.SemaphoreType.DMA((3, 2)),
                pltpu.SemaphoreType.DMA((3, nc)),
                pltpu.SemaphoreType.REGULAR,
            ],
            compiler_params=pltpu.CompilerParams(vmem_limit_bytes=VMEM_BYTES, collective_id=0, has_side_effects=True),
            cost_estimate=pl.CostEstimate(flops=8 * per_dev * rows * width * ff, bytes_accessed=2 * per_dev * width * ff, transcendentals=0),
            name="down",
        )(tab, act, w_down, shared)

    return jax.shard_map(device_fn, mesh=mesh, in_specs=(tok_spec, P(), bank_spec, bank_spec, bank_spec, P(), P(), P(), tok_spec, tok_spec), out_specs=tok_spec, check_vma=False)
```

time: 1270 us -> 427 us (0.34); the launches traced: 1250 us -> 425 us
  blocking collectives: 352 us -> 0 us
  Pallas kernels: 0 us -> 304 us
  local copies, waits for them, and re-layouts: 277 us -> 5.52 us
  waiting for transfers between devices: 300 us -> 54.2 us
  matrix products: 237 us -> 44 us
  other arithmetic: 82.1 us -> 0 us
  between operations: 0.26 us -> 13.4 us
    all_to_all x1 -> x0, blocking collectives: 352 us -> none  [device_fn(): recv_rows = lax.all_to_all(send_rows, 'ep', 1, 1, tiled=True)]
    pallas_call x0 -> x3, Pallas kernels: none -> 304 us  [the longest x1 165 us: device_fn(): pl.pallas_call(down_kernel, out_shape=jax.ShapeDtypeStruct((tokens, width...]
    all_to_all x1, waiting for transfers between devices: 300 us -> 0.01 us  [device_fn(): tab = lax.all_to_all(tab, 'ep', 0, 0, tiled=True)]
    dot_general x6 -> x2, matrix products: 237 us -> 44 us  [dot(): return jnp.dot(a, b, preferred_element_type=F32)]
    gather x8 -> x0, local copies, waits for them, and re-layouts: 193 us -> none  [the longest x2 135 us: device_fn(): jnp.take(back_rows.reshape(n_rows, hidden_dim), dest_row, axis=0, mode='f...]
    all_gather x0 -> x1, waiting for transfers between devices: none -> 53.5 us  [device_fn(): x_all = lax.all_gather(hidden, 'ep', axis=0, tiled=False)]
    all_to_all x2 -> x0, local copies, waits for them, and re-layouts: 43.4 us -> none  [the longest x1 21.7 us: device_fn(): lax.all_to_all(expert_out.reshape(per_dev, groups, capacity, hidden_dim),...]
    another operation x2 -> x0, other arithmetic: 32.1 us -> none
  transfers between devices with their start and end apart: 1 -> 2, of which waited for: 1 -> 1; matrix products, arithmetic and copies ran while one was open for 3% -> 11% of each run, Pallas kernels for 0% -> 1%
where the time goes in v1:
time: 427 us; the launch traced here: 425 us
  Pallas kernels  304 us (71%)
  waiting for transfers between devices  54.2 us (13%)
  matrix products  44 us (10%)
  between operations  13.4 us (3%)
  local copies, waits for them, and re-layouts  5.52 us (1%)
  starting transfers between devices  4.31 us (1%)
    pallas_call x1, Pallas kernels, device_fn(): pl.pallas_call(down_kernel, out_shape=jax.ShapeDtypeStruct((tokens, width...  165 us
    pallas_call x1, Pallas kernels, device_fn(): pl.pallas_call(up_kernel, out_shape=jax.ShapeDtypeStruct((per_dev, rows,...  135 us
    all_gather x1, waiting for transfers between devices, device_fn(): x_all = lax.all_gather(hidden, 'ep', axis=0, tiled=False)  53.5 us
    dot_general x2, matrix products, dot(): return jnp.dot(a, b, preferred_element_type=F32)  44 us
  transfers between devices with their start and end apart: 2, of which 1 were waited for; matrix products, arithmetic and copies ran while one was open for 11% of the time, Pallas kernels for 1%

profile of v1, /device:TPU:0, one launch (start us, length us, event | category | flops | bytes accessed | tf_op | source)
XLA Modules:
  0.0 425.1 jit_solution(542355879094907481)
XLA Ops:
  6.5 0.0 copy-start
  6.5 0.0 all-gather.3.cloned.1.call-start
  6.5 0.7 all-gather.3.cloned.1.call-update
  7.3 2.1 copy.11.w_ref
  9.4 3.7 route.1
  13.1 4.3 %all-to-all-start = ((f32[8,16,512]{2,1,0:T(8,128)}), f32[8,16,512]{2,1,0:T(8,128)}, u32[]{:S(2)}, u32[]{:S(2)}) async-start(f32[8,16,512]{2,1,0:T(8,128)} %route.1), calls=%async_computation | async-start | bytes 524288 | tf_op jit(solution)/shard_map/all_to_all | solution.py:335
  17.4 0.0 copy-done
  17.4 13.4 %fusion = f32[512,3072]{1,0:T(8,128)} fusion(bf16[512,2560]{1,0:T(8,128)(2,1)S(1)} %copy-done, bf16[2560,3072]{1,0:T(8,128)(2,1)} %param.15), kind=kOutput, calls=%fused_computation.1 | convolution fusion | flops 8053063680 | bytes 24641536 | tf_op jit(solution)/shard_map/dot_general | solution.py:19
  30.8 30.6 %fusion.1.ys_hbm = f32[512,2560]{1,0:T(8,128)} fusion(bf16[3072,2560]{1,0:T(8,128)(2,1)} %param.17, f32[512,3072]{1,0:T(8,128)} %fusion, bf16[512,2560]{1,0:T(8,128)(2,1)S(1)} %copy-done, bf16[2560,3072]{1,0:T(8,128)(2,1)} %param.16), kind=kOutput, calls=%fused_computation.2 | convolution fusion | flops 16115564544 | bytes 45613056 | tf_op jit(solution)/shard_map/dot_general | solution.py:19
  61.4 0.0 all-to-all-done.tab_ref
  61.4 53.5 %all-gather.3.cloned.1.call-done = bf16[4096,2560]{1,0:T(8,128)(2,1)} async-done(((bf16[512,2560]{1,0:T(8,128)(2,1)}), bf16[4096,2560]{1,0:T(8,128)(2,1)}) %all-gather.3.cloned.1.call-update) | async-done | bytes 20971536 | tf_op jit(solution)/shard_map/all_gather | solution.py:327
  114.9 134.6 %up.1.act_hbm = bf16[8,768,1536]{2,1,0:T(8,128)(2,1)} custom-call(f32[8,16,512]{2,1,0:T(8,128)} %all-to-all-done.tab_ref, bf16[8,512,2560]{2,1,0:T(8,128)(2,1)} %bitcast.19, bf16[8,2560,1536]{2,1,0:T(8,128)(2,1)} %w1_hbm.1, bf16[8,2560,1536]{2,1,0:T(8,128)(2,1)} %w3_hbm.1), custom_call_target="tpu_custom_call" | custom-call | flops 96636764160 | bytes 125829120 | tf_op jit(solution)/shard_map/up/pallas_call | solution.py:337
  249.5 165.4 %down.1 = bf16[512,2560]{1,0:T(8,128)(2,1)} custom-call(f32[8,16,512]{2,1,0:T(8,128)} %all-to-all-done.tab_ref, bf16[8,768,1536]{2,1,0:T(8,128)(2,1)} %up.1.act_hbm, bf16[8,1536,2560]{2,1,0:T(8,128)(2,1)} %w2_hbm.1, f32[512,2560]{1,0:T(8,128)} %fusion.1.ys_hbm), custom_call_target="tpu_custom_call" | custom-call | flops 193273528320 | bytes 62914560 | tf_op jit(solution)/shard_map/down/pallas_call | solution.py:357
  414.8 3.4 copy.13
Async XLA Ops:
  6.5 10.8 %copy-start = (bf16[512,2560]{1,0:T(8,128)(2,1)S(1)}, bf16[512,2560]{1,0:T(8,128)(2,1)}, u32[]{:S(2)}) copy-start(bf16[512,2560]{1,0:T(8,128)(2,1)} %x_ref.1) | copy-start | bytes 7864324
  6.5 108.3 %all-gather.3.cloned.1.call-start = ((), (), s32[]{:S(2)}) async-start(), calls=%async_computation.1 | async-start | bytes 23592960 | tf_op jit(solution)/shard_map/all_gather | solution.py:327
  13.1 48.3 %all-to-all-start = ((f32[8,16,512]{2,1,0:T(8,128)}), f32[8,16,512]{2,1,0:T(8,128)}, u32[]{:S(2)}, u32[]{:S(2)}) async-start(f32[8,16,512]{2,1,0:T(8,128)} %route.1), calls=%async_computation | async-start | bytes 524288 | tf_op jit(solution)/shard_map/all_to_all | solution.py:335
Sparse Core Ops, SparseCore 0:
  9.1 105.6 all-gather.2

commit v2 on v1

--- a/solution.py
+++ b/solution.py
@@ -17,13 +17,6 @@
 
 def dot(a, b):
     return jnp.dot(a, b, preferred_element_type=F32)
-
-
-def swiglu(tok_rows, gate_w, up_w, down_w):
-    h_gate = dot(tok_rows, gate_w)
-    h_up = dot(tok_rows, up_w)
-    act_rows = (jax.nn.silu(h_gate) * h_up).astype(BF16)
-    return dot(act_rows, down_w)
 
 
 def route_kernel(x_ref, w_ref, idx_ref, keep_ref, tab_ref):
@@ -46,83 +39,243 @@
         tab_ref[d, half:, :] = gate[d * half : (d + 1) * half]
 
 
-def up_kernel(tab_ref, x_hbm, w1_hbm, w3_hbm, act_hbm, xg, xbuf, dbuf, wg, wu, ab, x_sem, w_sem, a_sem):
-    groups, tokens, width = x_hbm.shape
+def relatives():
+    me = lax.axis_index("ep")
+    core, chip = lax.rem(me, 2), me // 2
+    yb, xb = chip // 2, lax.rem(chip, 2)
+
+    def first_core(r):
+        return 2 * (2 * lax.rem(yb + r // 2, 2) + lax.rem(xb + lax.rem(r, 2), 2))
+
+    return me, core, me + 1 - 2 * core, first_core
+
+
+def up_kernel(
+    tab_ref, x_hbm, w1_hbm, w3_hbm, sg_hbm, su_hbm, sd_hbm, tabs_ref, ys_hbm, act_hbm, x_all,
+    tabs, xown, xbuf, xg, dbuf, wg, wu, wd, hs, ab, yb,
+    own_sem, x_sem, w_sem, d_sem, a_sem, y_sem, ts_sem, tr_sem, xs_sem, xr_sem,
+):
+    groups = tabs.shape[0]
+    tokens, width = x_hbm.shape
     per_dev, _, ff = w1_hbm.shape
-    tn = wg.shape[2]
-    nt = ff // tn
+    slots, _, tn = wg.shape
+    nt, ns, nd = ff // tn, sg_hbm.shape[1] // tn, width // tn
     steps = per_dev * nt
     xc = 512
-
-    def x_copy(s, slot):
-        return pltpu.make_async_copy(x_hbm.at[s], xbuf.at[slot], x_sem.at[slot])
-
-    def w_copies(it, slot):
-        e, n = it // nt, lax.rem(it, nt)
+    early = 2 * CAP
+    late = groups * CAP - early
+    forward_at = (5 * steps) // 8
+
+    me, core, partner, first_core = relatives()
+
+    def block_copy(k, src, pos, device):
+        return pltpu.make_async_remote_copy(
+            src_ref=src, dst_ref=x_all.at[pos], send_sem=xs_sem.at[k], recv_sem=xr_sem.at[pos],
+            device_id={"ep": device}, device_id_type=MESH)
+
+    def table_copy(r, k):
+        dst = first_core(r) + k
+        return pltpu.make_async_remote_copy(
+            src_ref=tab_ref.at[dst], dst_ref=tabs.at[2 * r + core], send_sem=ts_sem.at[2 * r + k], recv_sem=tr_sem.at[2 * r + core],
+            device_id={"ep": dst}, device_id_type=MESH)
+
+    sends = [
+        block_copy(0, x_hbm, core, partner),
+        block_copy(1, x_hbm, 2 + core, first_core(1) + core),
+        block_copy(2, x_hbm, 4 + core, first_core(2) + core),
+        block_copy(3, x_all.at[2 + core], 2 + core, partner),
+        block_copy(4, x_all.at[4 + core], 4 + core, partner),
+        block_copy(5, x_all.at[4 - core], 6 + core, first_core(1 + core) + core),
+        block_copy(6, x_all.at[6 + core], 6 + core, partner),
+    ]
+
+    def arrived(pos):
+        block_copy(0, x_hbm, pos, partner).wait_recv()
+
+    def w_start(t):
+        slot = lax.rem(t, slots)
+
+        def go(a, b):
+            pltpu.make_async_copy(a, wg.at[slot], w_sem.at[0, slot]).start()
+            pltpu.make_async_copy(b, wu.at[slot], w_sem.at[1, slot]).start()
+
+        @pl.when(t < ns)
+        def _():
+            cols = pl.ds(pl.multiple_of(t * tn, tn), tn)
+            go(sg_hbm.at[:, cols], su_hbm.at[:, cols])
+
+        @pl.when((t >= ns) & (t < ns + 2 * steps))
+        def _():
+            it = lax.rem(t - ns, steps)
+            cols = pl.ds(pl.multiple_of(lax.rem(it, nt) * tn, tn), tn)
+            go(w1_hbm.at[it // nt, :, cols], w3_hbm.at[it // nt, :, cols])
+
+    def w_wait(t):
+        slot = lax.rem(t, slots)
+        pltpu.make_async_copy(sg_hbm.at[:, pl.ds(0, tn)], wg.at[slot], w_sem.at[0, slot]).wait()
+        pltpu.make_async_copy(sg_hbm.at[:, pl.ds(0, tn)], wu.at[slot], w_sem.at[1, slot]).wait()
+        return slot
+
+    def d_copy(n):
         cols = pl.ds(pl.multiple_of(n * tn, tn), tn)
-        return (
-            pltpu.make_async_copy(w1_hbm.at[e, :, cols], wg.at[slot], w_sem.at[0, slot]),
-            pltpu.make_async_copy(w3_hbm.at[e, :, cols], wu.at[slot], w_sem.at[1, slot]),
-        )
-
-    def a_copy(it, slot):
-        e, n = it // nt, lax.rem(it, nt)
+        return pltpu.make_async_copy(sd_hbm.at[:, cols], wd.at[lax.rem(n, 2)], d_sem.at[lax.rem(n, 2)])
+
+    def y_copy(n):
         cols = pl.ds(pl.multiple_of(n * tn, tn), tn)
-        return pltpu.make_async_copy(ab.at[slot], act_hbm.at[e, :, cols], a_sem.at[slot])
-
-    x_copy(0, 0).start()
-    for c in w_copies(0, 0):
-        c.start()
+        return pltpu.make_async_copy(yb.at[lax.rem(n, 2)], ys_hbm.at[:, cols], y_sem.at[lax.rem(n, 2)])
+
+    own_copy = pltpu.make_async_copy(x_hbm, xown, own_sem)
+    own_copy.start()
+    for t in range(slots - 1):
+        w_start(t)
+    d_copy(0).start()
+
+    barrier = pltpu.get_barrier_semaphore()
+    for d in range(1, groups):
+        pl.semaphore_signal(barrier, inc=1, device_id={"ep": lax.rem(me + d, groups)}, device_id_type=MESH)
+    pl.semaphore_wait(barrier, groups - 1)
+    for k in range(3):
+        sends[k].start()
+    for r in range(4):
+        for k in range(2):
+            if r == 0:
+                @pl.when(k != core)
+                def _():
+                    table_copy(r, k).start()
+            else:
+                table_copy(r, k).start()
+    tabs[core] = tab_ref[me]
+    own_copy.wait()
+
+    def shared_up(t, _):
+        w_start(t + slots - 1)
+        slot = w_wait(t)
+        h_gate = dot(xown[...], wg[slot])
+        h_up = dot(xown[...], wu[slot])
+        hs[:, pl.ds(pl.multiple_of(t * tn, tn), tn)] = (jax.nn.silu(h_gate) * h_up).astype(BF16)
+        return 0
+
+    lax.fori_loop(0, ns, shared_up, 0)
+
+    def shared_down(n, _):
+        slot = lax.rem(n, 2)
+
+        @pl.when(n + 1 < nd)
+        def _():
+            d_copy(n + 1).start()
+
+        d_copy(n).wait()
+
+        @pl.when(n >= 2)
+        def _():
+            y_copy(n - 2).wait()
+
+        yb[slot] = dot(hs[...], wd[slot])
+        y_copy(n).start()
+        return 0
+
+    lax.fori_loop(0, nd, shared_down, 0)
+    y_copy(nd - 2).wait()
+    y_copy(nd - 1).wait()
+
     row = lax.broadcasted_iota(jnp.int32, (CAP, tokens), 0).astype(F32)
 
-    def gather(s, _):
-        slot = lax.rem(s, 2)
-
-        @pl.when(s + 1 < groups)
-        def _():
-            x_copy(s + 1, 1 - slot).start()
-
+    def x_copy(pos, slot):
+        return pltpu.make_async_copy(x_all.at[pos], xbuf.at[slot], x_sem.at[slot])
+
+    def gather(pos, x_ref, base):
         for e in range(per_dev):
-            dbuf[e * CAP : (e + 1) * CAP, :] = jnp.where(row == tab_ref[s, e : e + 1, :], 1.0, 0.0).astype(BF16)
-        x_copy(s, slot).wait()
-        rows = pl.ds(pl.multiple_of(s * CAP, CAP), CAP)
+            dbuf[e * CAP : (e + 1) * CAP, :] = jnp.where(row == tabs[pos, pl.ds(e, 1), :], 1.0, 0.0).astype(BF16)
+        rows = pl.ds(pl.multiple_of(base, CAP), CAP)
 
         def cols_step(n, _):
             cols = pl.ds(pl.multiple_of(n * xc, xc), xc)
-            got = dot(dbuf[...], xbuf[slot, :, cols]).astype(BF16)
+            got = dot(dbuf[...], x_ref[:, cols]).astype(BF16)
             xg[:, rows, cols] = got.reshape(per_dev, CAP, xc)
             return 0
 
         lax.fori_loop(0, width // xc, cols_step, 0)
-        return 0
-
-    lax.fori_loop(0, groups, gather, 0)
-
-    def main(it, _):
+
+    def a_copy(it, n_rows, base):
+        cols = pl.ds(pl.multiple_of(lax.rem(it, nt) * tn, tn), tn)
         slot = lax.rem(it, 2)
-        e = it // nt
-
-        @pl.when(it + 1 < steps)
-        def _():
-            for c in w_copies(it + 1, 1 - slot):
-                c.start()
-
-        for c in w_copies(it, slot):
-            c.wait()
-
-        @pl.when(it >= 2)
-        def _():
-            a_copy(it - 2, slot).wait()
-
-        h_gate = dot(xg[e], wg[slot])
-        h_up = dot(xg[e], wu[slot])
-        ab[slot] = (jax.nn.silu(h_gate) * h_up).astype(BF16)
-        a_copy(it, slot).start()
-        return 0
-
-    lax.fori_loop(0, steps, main, 0)
-    a_copy(steps - 2, steps % 2).wait()
-    a_copy(steps - 1, (steps - 1) % 2).wait()
+        return pltpu.make_async_copy(ab.at[slot, pl.ds(0, n_rows)], act_hbm.at[it // nt, pl.ds(base, n_rows), cols], a_sem.at[slot])
+
+    def expert_pass(first, n_rows, base):
+        def body(it, _):
+            t = first + it
+            w_start(t + slots - 1)
+            slot = w_wait(t)
+
+            @pl.when(it >= 2)
+            def _():
+                a_copy(it - 2, n_rows, base).wait()
+
+            e = it // nt
+            h_gate = dot(xg[e, :n_rows], wg[slot])
+            h_up = dot(xg[e, :n_rows], wu[slot])
+            ab[lax.rem(it, 2), :n_rows] = (jax.nn.silu(h_gate) * h_up).astype(BF16)
+            a_copy(it, n_rows, base).start()
+
+            if base == 0:
+                @pl.when(it == forward_at)
+                def _():
+                    arrived(2 + core)
+                    sends[3].start()
+                    arrived(4 + core)
+                    sends[4].start()
+                    sends[5].start()
+
+            return 0
+
+        lax.fori_loop(0, steps, body, 0)
+        a_copy(steps - 2, n_rows, base).wait()
+        a_copy(steps - 1, n_rows, base).wait()
+
+    for p in range(groups):
+        @pl.when(p != core)
+        def _():
+            pltpu.make_async_remote_copy(
+                src_ref=tab_ref.at[0], dst_ref=tabs.at[p], send_sem=ts_sem.at[p], recv_sem=tr_sem.at[p],
+                device_id={"ep": partner}, device_id_type=MESH).wait_recv()
+
+    arrived(1 - core)
+    x_copy(1 - core, 0).start()
+    gather(core, xown, core * CAP)
+    x_copy(1 - core, 0).wait()
+    gather(1 - core, xbuf.at[0], (1 - core) * CAP)
+    expert_pass(ns, early, 0)
+
+    order = [2 + core, 4 + core, 3 - core, 5 - core, 6 + core, 7 - core]
+    x_copy(order[0], 0).start()
+    x_copy(order[1], 1).start()
+    for n, pos in enumerate(order):
+        x_copy(pos, n % 2).wait()
+        gather(pos, xbuf.at[n % 2], (pos - 2) * CAP)
+        if n + 2 < 6:
+            if n + 2 == 2:
+                arrived(3 - core)
+            if n + 2 == 3:
+                arrived(5 - core)
+            if n + 2 == 5:
+                arrived(7 - core)
+            if n + 2 == 4:
+                arrived(6 + core)
+                sends[6].start()
+            x_copy(order[n + 2], n % 2).start()
+    expert_pass(ns + steps, late, early)
+
+    for k in range(7):
+        sends[k].wait_send()
+    for r in range(4):
+        for k in range(2):
+            if r == 0:
+                @pl.when(k != core)
+                def _():
+                    table_copy(r, k).wait_send()
+            else:
+                table_copy(r, k).wait_send()
+    tabs_ref[...] = tabs[...]
 
 
 def down_kernel(
@@ -137,14 +290,7 @@
     nc = acc.shape[0]
     steps = 4 * nc
 
-    me = lax.axis_index("ep")
-    core, chip = lax.rem(me, 2), me // 2
-    partner = me + 1 - 2 * core
-    yb, xb = chip // 2, lax.rem(chip, 2)
-
-    def chip_at(j):
-        m = 3 - j
-        return 2 * lax.rem(yb + m // 2, 2) + lax.rem(xb + lax.rem(m, 2), 2)
+    me, core, partner, first_core = relatives()
 
     def w_copy(it, slot):
         c, e = it // per_dev, lax.rem(it, per_dev)
@@ -166,7 +312,7 @@
     barrier = pltpu.get_barrier_semaphore()
     pl.semaphore_signal(barrier, inc=1, device_id={"ep": partner}, device_id_type=MESH)
     for j in range(3):
-        pl.semaphore_signal(barrier, inc=1, device_id={"ep": 2 * chip_at(j) + core}, device_id_type=MESH)
+        pl.semaphore_signal(barrier, inc=1, device_id={"ep": first_core(3 - j) + core}, device_id_type=MESH)
     pl.semaphore_wait(barrier, 4)
 
     lane = lax.broadcasted_iota(jnp.int32, (per_dev, rows), 1)
@@ -202,7 +348,7 @@
         slot = lax.rem(c, 2)
         return pltpu.make_async_remote_copy(
             src_ref=bsend.at[j, slot], dst_ref=brecv.at[j, c], send_sem=bs_sem.at[j, slot], recv_sem=br_sem.at[j, c],
-            device_id={"ep": 2 * chip_at(j) + core}, device_id_type=MESH)
+            device_id={"ep": first_core(3 - j) + core}, device_id_type=MESH)
 
     def combine(s):
         return dot(comb[0, s], part[s]) + dot(comb[1, s], part[s]) + dot(comb[2, s], part[s])
@@ -258,14 +404,14 @@
         def pair_step(j, _):
             g = 4 * c + j
             slot = lax.rem(g, 2)
-            q = chip_at(j)
+            p = 2 * (3 - j)
 
             @pl.when(g >= 2)
             def _():
                 f_copy(slot).wait_send()
 
-            fsend[slot] = combine(2 * q + 1 - core)
-            mine[slot] = combine(2 * q + core)
+            fsend[slot] = combine(p + 1 - core)
+            mine[slot] = combine(p + core)
 
             @pl.when(g >= 2)
             def _():
@@ -324,7 +470,6 @@
         rows = groups * CAP
         tn, cw = 256, 256
         nc = width // cw
-        x_all = lax.all_gather(hidden, "ep", axis=0, tiled=False)
         tab = pl.pallas_call(
             route_kernel,
             out_shape=jax.ShapeDtypeStruct((groups, 2 * per_dev, tokens), F32),
@@ -332,28 +477,44 @@
             out_specs=vmem,
             name="route",
         )(hidden, w_router, top_idx.T, keep_mask.T)
-        tab = lax.all_to_all(tab, "ep", 0, 0, tiled=True)
-        shared = swiglu(hidden, shared_gate, shared_up, shared_down)
-        act = pl.pallas_call(
+        sff = shared_gate.shape[1]
+        slots = 4
+        tabs, shared, act, _ = pl.pallas_call(
             up_kernel,
-            out_shape=jax.ShapeDtypeStruct((per_dev, rows, ff), BF16),
-            in_specs=[vmem, hbm, hbm, hbm],
-            out_specs=hbm,
+            out_shape=(
+                jax.ShapeDtypeStruct(tab.shape, F32),
+                jax.ShapeDtypeStruct((tokens, width), F32),
+                jax.ShapeDtypeStruct((per_dev, rows, ff), BF16),
+                jax.ShapeDtypeStruct((groups, tokens, width), BF16),
+            ),
+            in_specs=[vmem] + [hbm] * 6,
+            out_specs=(vmem, hbm, hbm, hbm),
             scratch_shapes=[
-                pltpu.VMEM((per_dev, rows, width), BF16),
+                pltpu.VMEM(tab.shape, F32),
+                pltpu.VMEM((tokens, width), BF16),
                 pltpu.VMEM((2, tokens, width), BF16),
+                pltpu.VMEM((per_dev, rows - 2 * CAP, width), BF16),
                 pltpu.VMEM((per_dev * CAP, tokens), BF16),
-                pltpu.VMEM((2, width, tn), BF16),
-                pltpu.VMEM((2, width, tn), BF16),
-                pltpu.VMEM((2, rows, tn), BF16),
-                pltpu.SemaphoreType.DMA((2,)),
-                pltpu.SemaphoreType.DMA((2, 2)),
-                pltpu.SemaphoreType.DMA((2,)),
+                pltpu.VMEM((slots, width, tn), BF16),
+                pltpu.VMEM((slots, width, tn), BF16),
+                pltpu.VMEM((2, sff, tn), BF16),
+                pltpu.VMEM((tokens, sff), BF16),
+                pltpu.VMEM((2, rows - 2 * CAP, tn), BF16),
+                pltpu.VMEM((2, tokens, tn), F32),
+                pltpu.SemaphoreType.DMA,
+                pltpu.SemaphoreType.DMA((2,)),
+                pltpu.SemaphoreType.DMA((2, slots)),
+                pltpu.SemaphoreType.DMA((2,)),
+                pltpu.SemaphoreType.DMA((2,)),
+                pltpu.SemaphoreType.DMA((2,)),
+                pltpu.SemaphoreType.DMA((groups,)),
+                pltpu.SemaphoreType.DMA((groups,)),
+                pltpu.SemaphoreType.DMA((7,)),
+                pltpu.SemaphoreType.DMA((groups,)),
             ],
-            compiler_params=pltpu.CompilerParams(vmem_limit_bytes=VMEM_BYTES),
-            cost_estimate=pl.CostEstimate(flops=4 * per_dev * rows * width * ff, bytes_accessed=4 * per_dev * width * ff, transcendentals=0),
+            compiler_params=pltpu.CompilerParams(vmem_limit_bytes=VMEM_BYTES, collective_id=1, has_side_effects=True),
             name="up",
-        )(tab, x_all, w_gate, w_up)
+        )(tab, hidden, w_gate, w_up, shared_gate, shared_up, shared_down)
         return pl.pallas_call(
             down_kernel,
             out_shape=jax.ShapeDtypeStruct((tokens, width), BF16),
@@ -384,6 +545,6 @@
             compiler_params=pltpu.CompilerParams(vmem_limit_bytes=VMEM_BYTES, collective_id=0, has_side_effects=True),
             cost_estimate=pl.CostEstimate(flops=8 * per_dev * rows * width * ff, bytes_accessed=2 * per_dev * width * ff, transcendentals=0),
             name="down",
-        )(tab, act, w_down, shared)
+        )(tabs, act, w_down, shared)
 
     return jax.shard_map(device_fn, mesh=mesh, in_specs=(tok_spec, P(), bank_spec, bank_spec, bank_spec, P(), P(), P(), tok_spec, tok_spec), out_specs=tok_spec, check_vma=False)

time: 427 us -> 400 us (0.937)
  Pallas kernels: 304 us -> 392 us
  waiting for transfers between devices: 54.2 us -> 0 us
  matrix products: 44 us -> 0 us
  between operations: 13.4 us -> 0.02 us
  starting transfers between devices: 4.31 us -> 0 us
    pallas_call x1, Pallas kernels: 135 us -> 222 us  [device_fn(): pl.pallas_call(up_kernel, out_shape=(jax.ShapeDtypeStruct(tab.shape, F32)...]
    all_gather x1 -> x0, waiting for transfers between devices: 53.5 us -> none  [device_fn(): x_all = lax.all_gather(hidden, 'ep', axis=0, tiled=False)]
    dot_general x2 -> x0, matrix products: 44 us -> none  [dot(): return jnp.dot(a, b, preferred_element_type=F32)]
    all_to_all x1 -> x0, starting transfers between devices: 4.31 us -> none  [device_fn(): tab = lax.all_to_all(tab, 'ep', 0, 0, tiled=True)]
  transfers between devices with their start and end apart: 2 -> 0, of which waited for: 1 -> 0; matrix products, arithmetic and copies ran while one was open for 11% -> 0% of each run, Pallas kernels for 1% -> 0%
where the time goes in v2:
time: 400 us; the launch traced here: 398 us
  Pallas kernels  392 us (98%)
  local copies, waits for them, and re-layouts  5.45 us (1%)
    pallas_call x1, Pallas kernels, device_fn(): pl.pallas_call(up_kernel, out_shape=(jax.ShapeDtypeStruct(tab.shape, F32)...  222 us
    pallas_call x1, Pallas kernels, device_fn(): pl.pallas_call(down_kernel, out_shape=jax.ShapeDtypeStruct((tokens, width...  166 us

profile of v2, /device:TPU:0, one launch (start us, length us, event | category | flops | bytes accessed | tf_op | source)
XLA Modules:
  0.0 397.7 jit_solution(600621421913060697)
XLA Ops:
  0.0 2.1 copy.11.w_ref
  2.1 3.7 route.1.tab_ref
  5.7 222.2 %up.1 = (f32[8,16,512]{2,1,0:T(8,128)}, f32[512,2560]{1,0:T(8,128)}, bf16[8,768,1536]{2,1,0:T(8,128)(2,1)}, bf16[8,512,2560]{2,1,0:T(8,128)(2,1)}) custom-call(f32[8,16,512]{2,1,0:T(8,128)} %route.1.tab_ref, bf16[512,2560]{1,0:T(8,128)(2,1)} %x_hbm.1, bf16[8,2560,1536]{2,1,0:T(8,128)(2,1)} %w1_hbm.1, bf16[8,2560,1536]{2,1,0:T(8,128)(2,1)} %w3_hbm.1, ...), custom_call_target="tpu_custom_call" | custom-call | tf_op jit(solution)/shard_map/up/pallas_call | solution.py:482
  228.0 166.3 %down.1 = bf16[512,2560]{1,0:T(8,128)(2,1)} custom-call(f32[8,16,512]{2,1,0:T(8,128)} %get-tuple-element.8.tab_ref, bf16[8,768,1536]{2,1,0:T(8,128)(2,1)} %get-tuple-element.9.act_hbm, bf16[8,1536,2560]{2,1,0:T(8,128)(2,1)} %w2_hbm.1, f32[512,2560]{1,0:T(8,128)} %get-tuple-element.10.ys_hbm), custom_call_target="tpu_custom_call" | custom-call | flops 193273528320 | bytes 62914560 | tf_op jit(solution)/shard_map/down/pallas_call | solution.py:518
  394.3 3.4 copy.13

commit v3 on v2

--- a/solution.py
+++ b/solution.py
@@ -20,8 +20,8 @@
 
 
 def route_kernel(x_ref, w_ref, idx_ref, keep_ref, tab_ref):
-    experts, tokens = w_ref.shape[1], x_ref.shape[0]
-    logits = lax.dot_general(w_ref[...], x_ref[...], (((0,), (1,)), ((), ())), preferred_element_type=F32)
+    experts, tokens = w_ref.shape[0], x_ref.shape[0]
+    logits = lax.dot_general(w_ref[...], x_ref[...], (((1,), (1,)), ((), ())), preferred_element_type=F32)
     e = jnp.exp(logits - jnp.max(logits, axis=0, keepdims=True))
     prob = e / jnp.sum(e, axis=0, keepdims=True)
     expert_id = lax.broadcasted_iota(jnp.int32, (experts, tokens), 0)
@@ -52,7 +52,7 @@
 
 def up_kernel(
     tab_ref, x_hbm, w1_hbm, w3_hbm, sg_hbm, su_hbm, sd_hbm, tabs_ref, ys_hbm, act_hbm, x_all,
-    tabs, xown, xbuf, xg, dbuf, wg, wu, wd, hs, ab, yb,
+    tabs, xown, xbuf, xg, dbuf, wg, wu, wd, hs, hg, hu, ab, yb,
     own_sem, x_sem, w_sem, d_sem, a_sem, y_sem, ts_sem, tr_sem, xs_sem, xr_sem,
 ):
     groups = tabs.shape[0]
@@ -61,10 +61,10 @@
     slots, _, tn = wg.shape
     nt, ns, nd = ff // tn, sg_hbm.shape[1] // tn, width // tn
     steps = per_dev * nt
-    xc = 512
+    xc = width // 2
     early = 2 * CAP
     late = groups * CAP - early
-    forward_at = (5 * steps) // 8
+    forward_at = steps // 2
 
     me, core, partner, first_core = relatives()
 
@@ -118,7 +118,7 @@
 
     def d_copy(n):
         cols = pl.ds(pl.multiple_of(n * tn, tn), tn)
-        return pltpu.make_async_copy(sd_hbm.at[:, cols], wd.at[lax.rem(n, 2)], d_sem.at[lax.rem(n, 2)])
+        return pltpu.make_async_copy(sd_hbm.at[:, cols], wd.at[lax.rem(n, 3)], d_sem.at[lax.rem(n, 3)])
 
     def y_copy(n):
         cols = pl.ds(pl.multiple_of(n * tn, tn), tn)
@@ -129,13 +129,12 @@
     for t in range(slots - 1):
         w_start(t)
     d_copy(0).start()
+    d_copy(1).start()
 
     barrier = pltpu.get_barrier_semaphore()
     for d in range(1, groups):
         pl.semaphore_signal(barrier, inc=1, device_id={"ep": lax.rem(me + d, groups)}, device_id_type=MESH)
     pl.semaphore_wait(barrier, groups - 1)
-    for k in range(3):
-        sends[k].start()
     for r in range(4):
         for k in range(2):
             if r == 0:
@@ -144,25 +143,54 @@
                     table_copy(r, k).start()
             else:
                 table_copy(r, k).start()
+    for k in range(3):
+        sends[k].start()
     tabs[core] = tab_ref[me]
     own_copy.wait()
 
-    def shared_up(t, _):
-        w_start(t + slots - 1)
-        slot = w_wait(t)
-        h_gate = dot(xown[...], wg[slot])
-        h_up = dot(xown[...], wu[slot])
-        hs[:, pl.ds(pl.multiple_of(t * tn, tn), tn)] = (jax.nn.silu(h_gate) * h_up).astype(BF16)
-        return 0
-
-    lax.fori_loop(0, ns, shared_up, 0)
+    def gated_pass(first, n_steps, n_rows, lhs, before, after):
+        def activate(h):
+            return (jax.nn.silu(hg[h, :n_rows]) * hu[h, :n_rows]).astype(BF16)
+
+        def body(i, _):
+            for h in range(2):
+                it = 2 * i + h
+                w_start(first + it + slots - 1)
+                slot = w_wait(first + it)
+                last = it - 1
+                before(last)
+                ab[1 - h, :n_rows] = activate(1 - h)
+                x = lhs(it)
+                hg[h, :n_rows] = dot(x, wg[slot])
+                hu[h, :n_rows] = dot(x, wu[slot])
+                after(last)
+            return 0
+
+        lax.fori_loop(0, n_steps // 2, body, 0)
+        before(n_steps - 1)
+        ab[1, :n_rows] = activate(1)
+        after(n_steps - 1)
+
+    def s_copy(it):
+        cols = pl.ds(pl.multiple_of(it * tn, tn), tn)
+        return ab.at[lax.rem(it, 2), pl.ds(0, tokens)], hs.at[:, cols]
+
+    def shared_after(it):
+        @pl.when(it >= 0)
+        def _():
+            src, dst = s_copy(it)
+            dst[...] = src[...]
+
+    hg[...] = jnp.zeros_like(hg)
+    hu[...] = jnp.zeros_like(hu)
+    gated_pass(0, ns, tokens, lambda it: xown[...], lambda it: None, shared_after)
 
     def shared_down(n, _):
         slot = lax.rem(n, 2)
 
-        @pl.when(n + 1 < nd)
-        def _():
-            d_copy(n + 1).start()
+        @pl.when(n + 2 < nd)
+        def _():
+            d_copy(n + 2).start()
 
         d_copy(n).wait()
 
@@ -170,7 +198,7 @@
         def _():
             y_copy(n - 2).wait()
 
-        yb[slot] = dot(hs[...], wd[slot])
+        yb[slot] = dot(hs[...], wd[lax.rem(n, 3)])
         y_copy(n).start()
         return 0
 
@@ -202,20 +230,15 @@
         return pltpu.make_async_copy(ab.at[slot, pl.ds(0, n_rows)], act_hbm.at[it // nt, pl.ds(base, n_rows), cols], a_sem.at[slot])
 
     def expert_pass(first, n_rows, base):
-        def body(it, _):
-            t = first + it
-            w_start(t + slots - 1)
-            slot = w_wait(t)
-
+        def before(it):
             @pl.when(it >= 2)
             def _():
                 a_copy(it - 2, n_rows, base).wait()
 
-            e = it // nt
-            h_gate = dot(xg[e, :n_rows], wg[slot])
-            h_up = dot(xg[e, :n_rows], wu[slot])
-            ab[lax.rem(it, 2), :n_rows] = (jax.nn.silu(h_gate) * h_up).astype(BF16)
-            a_copy(it, n_rows, base).start()
+        def after(it):
+            @pl.when(it >= 0)
+            def _():
+                a_copy(it, n_rows, base).start()
 
             if base == 0:
                 @pl.when(it == forward_at)
@@ -226,9 +249,7 @@
                     sends[4].start()
                     sends[5].start()
 
-            return 0
-
-        lax.fori_loop(0, steps, body, 0)
+        gated_pass(first, steps, n_rows, lambda it: xg[it // nt, :n_rows], before, after)
         a_copy(steps - 2, n_rows, base).wait()
         a_copy(steps - 1, n_rows, base).wait()
 
@@ -292,7 +313,8 @@
 
     me, core, partner, first_core = relatives()
 
-    def w_copy(it, slot):
+    def w_copy(it):
+        slot = lax.rem(it, 4)
         c, e = it // per_dev, lax.rem(it, per_dev)
         cols = pl.ds(pl.multiple_of(c * cw, cw), cw)
         return pltpu.make_async_copy(w2_hbm.at[e, :, cols], wbuf.at[slot], w_sem.at[slot])
@@ -303,7 +325,8 @@
     def acc_copy(c):
         return pltpu.make_async_copy(ys_hbm.at[:, pl.ds(c * cw, cw)], acc.at[c], acc_sem.at[c])
 
-    w_copy(0, 0).start()
+    for it in range(2):
+        w_copy(it).start()
     for e in range(per_dev):
         act_copy(e).start()
     for c in range(nc):
@@ -324,7 +347,7 @@
     def over_slots(v):
         return lax.dot_general(v, spread, (((0,), (0,)), ((), ())), preferred_element_type=F32)
 
-    def build(s, _):
+    def build(s):
         hit = over_slots(tab_ref[s, :per_dev, :].astype(BF16)) == want
         gate = tab_ref[s, per_dev:, :]
         hi = gate.astype(BF16)
@@ -332,10 +355,8 @@
         mid = rest.astype(BF16)
         low = (rest - mid.astype(F32)).astype(BF16)
         for k, piece in enumerate((hi, mid, low)):
-            comb[k, s] = jnp.where(hit, over_slots(piece), 0.0).astype(BF16)
-        return 0
-
-    lax.fori_loop(0, groups, build, 0)
+            comb[s, k * tokens : (k + 1) * tokens] = jnp.where(hit, over_slots(piece), 0.0).astype(BF16)
+
     for c in range(nc):
         acc_copy(c).wait()
 
@@ -351,7 +372,8 @@
             device_id={"ep": first_core(3 - j) + core}, device_id_type=MESH)
 
     def combine(s):
-        return dot(comb[0, s], part[s]) + dot(comb[1, s], part[s]) + dot(comb[2, s], part[s])
+        pieces = dot(comb[s], part[s])
+        return pieces[:tokens] + pieces[tokens : 2 * tokens] + pieces[2 * tokens :]
 
     def launch(h):
         j = lax.rem(h, 4)
@@ -361,7 +383,7 @@
             b_copy(j, h // 4).start()
 
     def consume(h):
-        slot, c, j = lax.rem(h, 2), h // 4, lax.rem(h, 4)
+        slot, c, j = lax.rem(h, 3), h // 4, lax.rem(h, 4)
         f_copy(slot).wait_recv()
 
         @pl.when(j < 3)
@@ -376,56 +398,65 @@
         def _():
             acc[c] = acc[c] + (mine[slot] + frecv[slot])
 
-        @pl.when(h + 2 < steps)
+        @pl.when(h + 3 < steps)
         def _():
             pl.semaphore_signal(credit, inc=1, device_id={"ep": partner}, device_id_type=MESH)
 
     def chunk(c, _):
-        def down(e, _):
-            it = c * per_dev + e
-            slot = lax.rem(it, 2)
-
-            @pl.when(it + 1 < nc * per_dev)
-            def _():
-                w_copy(it + 1, 1 - slot).start()
-
-            w_copy(it, slot).wait()
-
-            @pl.when(c == 0)
-            def _():
-                act_copy(e).wait()
-
-            got = dot(act[e], wbuf[slot]).astype(BF16)
-            part[:, pl.ds(pl.multiple_of(e * CAP, CAP), CAP), :] = got.reshape(groups, CAP, cw)
+        def down(i, _):
+            for h in range(2):
+                it = c * per_dev + 2 * i + h
+
+                @pl.when(it + 2 < nc * per_dev)
+                def _():
+                    w_copy(it + 2).start()
+
+                @pl.when(c == 0)
+                def _():
+                    act_copy(2 * i + h).wait()
+
+            for h in range(2):
+                w_copy(c * per_dev + 2 * i + h).wait()
+            got = []
+            for h in range(2):
+                it = c * per_dev + 2 * i + h
+                got.append(dot(act[2 * i + h], wbuf[lax.rem(it, 4)]).astype(BF16))
+            for h in range(2):
+                part[:, pl.ds(pl.multiple_of((2 * i + h) * CAP, CAP), CAP), :] = got[h].reshape(groups, CAP, cw)
             return 0
 
-        lax.fori_loop(0, per_dev, down, 0)
+        lax.fori_loop(0, per_dev // 2, down, 0)
 
         def pair_step(j, _):
             g = 4 * c + j
-            slot = lax.rem(g, 2)
+            slot = lax.rem(g, 3)
             p = 2 * (3 - j)
 
-            @pl.when(g >= 2)
+            @pl.when(c == 0)
+            def _():
+                build(p)
+                build(p + 1)
+
+            @pl.when(g >= 3)
             def _():
                 f_copy(slot).wait_send()
 
             fsend[slot] = combine(p + 1 - core)
             mine[slot] = combine(p + core)
 
+            @pl.when(g >= 3)
+            def _():
+                pl.semaphore_wait(credit, 1)
+
+            f_copy(slot).start()
+
+            @pl.when(g >= 3)
+            def _():
+                launch(g - 3)
+
             @pl.when(g >= 2)
             def _():
-                pl.semaphore_wait(credit, 1)
-
-            f_copy(slot).start()
-
-            @pl.when(g >= 2)
-            def _():
-                launch(g - 2)
-
-            @pl.when(g >= 1)
-            def _():
-                consume(g - 1)
+                consume(g - 2)
 
             return 0
 
@@ -433,10 +464,12 @@
         return 0
 
     lax.fori_loop(0, nc, chunk, 0)
+    launch(steps - 3)
+    consume(steps - 2)
     launch(steps - 2)
     consume(steps - 1)
-    f_copy(0).wait_send()
-    f_copy(1).wait_send()
+    for slot in range(3):
+        f_copy(slot).wait_send()
 
     def y_copy(c):
         return pltpu.make_async_copy(ybuf.at[c % 2], y_hbm.at[:, pl.ds(c * cw, cw)], y_sem.at[c % 2])
@@ -476,7 +509,7 @@
             in_specs=[vmem] * 4,
             out_specs=vmem,
             name="route",
-        )(hidden, w_router, top_idx.T, keep_mask.T)
+        )(hidden, w_router.T, top_idx.T, keep_mask.T)
         sff = shared_gate.shape[1]
         slots = 4
         tabs, shared, act, _ = pl.pallas_call(
@@ -497,14 +530,16 @@
                 pltpu.VMEM((per_dev * CAP, tokens), BF16),
                 pltpu.VMEM((slots, width, tn), BF16),
                 pltpu.VMEM((slots, width, tn), BF16),
-                pltpu.VMEM((2, sff, tn), BF16),
+                pltpu.VMEM((3, sff, tn), BF16),
                 pltpu.VMEM((tokens, sff), BF16),
+                pltpu.VMEM((2, rows - 2 * CAP, tn), F32),
+                pltpu.VMEM((2, rows - 2 * CAP, tn), F32),
                 pltpu.VMEM((2, rows - 2 * CAP, tn), BF16),
                 pltpu.VMEM((2, tokens, tn), F32),
                 pltpu.SemaphoreType.DMA,
                 pltpu.SemaphoreType.DMA((2,)),
                 pltpu.SemaphoreType.DMA((2, slots)),
-                pltpu.SemaphoreType.DMA((2,)),
+                pltpu.SemaphoreType.DMA((3,)),
                 pltpu.SemaphoreType.DMA((2,)),
                 pltpu.SemaphoreType.DMA((2,)),
                 pltpu.SemaphoreType.DMA((groups,)),
@@ -521,23 +556,23 @@
             in_specs=[vmem, hbm, hbm, hbm],
             out_specs=hbm,
             scratch_shapes=[
-                pltpu.VMEM((3, groups, tokens, per_dev * CAP), BF16),
+                pltpu.VMEM((groups, 3 * tokens, per_dev * CAP), BF16),
                 pltpu.VMEM((per_dev, rows, ff), BF16),
                 pltpu.VMEM((groups, per_dev * CAP, cw), BF16),
-                pltpu.VMEM((2, ff, cw), BF16),
-                pltpu.VMEM((2, tokens, cw), F32),
-                pltpu.VMEM((2, tokens, cw), F32),
-                pltpu.VMEM((2, tokens, cw), F32),
+                pltpu.VMEM((4, ff, cw), BF16),
+                pltpu.VMEM((3, tokens, cw), F32),
+                pltpu.VMEM((3, tokens, cw), F32),
+                pltpu.VMEM((3, tokens, cw), F32),
                 pltpu.VMEM((3, 2, tokens, cw), BF16),
                 pltpu.VMEM((3, nc, tokens, cw), BF16),
                 pltpu.VMEM((nc, tokens, cw), F32),
                 pltpu.VMEM((2, tokens, cw), BF16),
                 pltpu.SemaphoreType.DMA((per_dev,)),
-                pltpu.SemaphoreType.DMA((2,)),
+                pltpu.SemaphoreType.DMA((4,)),
                 pltpu.SemaphoreType.DMA((nc,)),
                 pltpu.SemaphoreType.DMA((2,)),
-                pltpu.SemaphoreType.DMA((2,)),
-                pltpu.SemaphoreType.DMA((2,)),
+                pltpu.SemaphoreType.DMA((3,)),
+                pltpu.SemaphoreType.DMA((3,)),
                 pltpu.SemaphoreType.DMA((3, 2)),
                 pltpu.SemaphoreType.DMA((3, nc)),
                 pltpu.SemaphoreType.REGULAR,

time: 400 us -> 351 us (0.88)
  Pallas kernels: 392 us -> 347 us
    pallas_call x1, Pallas kernels: 222 us -> 192 us  [device_fn(): pl.pallas_call(up_kernel, out_shape=(jax.ShapeDtypeStruct(tab.shape, F32)...]
    pallas_call x1, Pallas kernels: 166 us -> 152 us  [device_fn(): pl.pallas_call(down_kernel, out_shape=jax.ShapeDtypeStruct((tokens, width...]
where the time goes in v3:
time: 351 us
  Pallas kernels  347 us (99%)
    pallas_call x1, Pallas kernels, device_fn(): pl.pallas_call(up_kernel, out_shape=(jax.ShapeDtypeStruct(tab.shape, F32)...  192 us
    pallas_call x1, Pallas kernels, device_fn(): pl.pallas_call(down_kernel, out_shape=jax.ShapeDtypeStruct((tokens, width...  152 us

profile of v3, /device:TPU:0, one launch (start us, length us, event | category | flops | bytes accessed | tf_op | source)
XLA Modules:
  0.0 350.7 jit_solution(9023601963074285371)
XLA Ops:
  0.0 3.6 %route.1.tab_ref = f32[8,16,512]{2,1,0:T(8,128)} custom-call(bf16[512,2560]{1,0:T(8,128)(2,1)} %x_hbm.1, bf16[64,2560]{1,0:T(8,128)(2,1)} %bitcast.3, s32[6,512]{1,0:T(8,128)} %bitcast.4, s32[6,512]{1,0:T(8,128)} %bitcast.5), custom_call_target="tpu_custom_call" | custom-call | tf_op jit(solution)/shard_map/route/pallas_call | solution.py:506
  3.6 191.8 %up.1 = (f32[8,16,512]{2,1,0:T(8,128)}, f32[512,2560]{1,0:T(8,128)}, bf16[8,768,1536]{2,1,0:T(8,128)(2,1)}, bf16[8,512,2560]{2,1,0:T(8,128)(2,1)}) custom-call(f32[8,16,512]{2,1,0:T(8,128)} %route.1.tab_ref, bf16[512,2560]{1,0:T(8,128)(2,1)} %x_hbm.1, bf16[8,2560,1536]{2,1,0:T(8,128)(2,1)} %w1_hbm.1, bf16[8,2560,1536]{2,1,0:T(8,128)(2,1)} %w3_hbm.1, ...), custom_call_target="tpu_custom_call" | custom-call | tf_op jit(solution)/shard_map/up/pallas_call | solution.py:515
  195.4 151.8 %down.1 = bf16[512,2560]{1,0:T(8,128)(2,1)} custom-call(f32[8,16,512]{2,1,0:T(8,128)} %get-tuple-element.8.tab_ref, bf16[8,768,1536]{2,1,0:T(8,128)(2,1)} %get-tuple-element.9.act_hbm, bf16[8,1536,2560]{2,1,0:T(8,128)(2,1)} %w2_hbm.1, f32[512,2560]{1,0:T(8,128)} %get-tuple-element.10.ys_hbm), custom_call_target="tpu_custom_call" | custom-call | flops 193273528320 | bytes 62914560 | tf_op jit(solution)/shard_map/down/pallas_call | solution.py:553
  347.3 3.4 copy.12

commit v4 on v3

--- a/solution.py
+++ b/solution.py
@@ -19,9 +19,9 @@
     return jnp.dot(a, b, preferred_element_type=F32)
 
 
-def route_kernel(x_ref, w_ref, idx_ref, keep_ref, tab_ref):
-    experts, tokens = w_ref.shape[0], x_ref.shape[0]
-    logits = lax.dot_general(w_ref[...], x_ref[...], (((1,), (1,)), ((), ())), preferred_element_type=F32)
+def route(x, w, idx_ref, keep_ref, tab_ref):
+    experts, tokens = w.shape[0], x.shape[0]
+    logits = lax.dot_general(w, x, (((1,), (1,)), ((), ())), preferred_element_type=F32)
     e = jnp.exp(logits - jnp.max(logits, axis=0, keepdims=True))
     prob = e / jnp.sum(e, axis=0, keepdims=True)
     expert_id = lax.broadcasted_iota(jnp.int32, (experts, tokens), 0)
@@ -51,9 +51,9 @@
 
 
 def up_kernel(
-    tab_ref, x_hbm, w1_hbm, w3_hbm, sg_hbm, su_hbm, sd_hbm, tabs_ref, ys_hbm, act_hbm, x_all,
-    tabs, xown, xbuf, xg, dbuf, wg, wu, wd, hs, hg, hu, ab, yb,
-    own_sem, x_sem, w_sem, d_sem, a_sem, y_sem, ts_sem, tr_sem, xs_sem, xr_sem,
+    wr_ref, idx_ref, keep_ref, x_hbm, w1_hbm, w3_hbm, sg_hbm, su_hbm, sd_hbm, comb_hbm, ys_hbm, act_hbm, x_all,
+    tab_ref, tabs, cbuf, xown, xbuf, xg, dbuf, wg, wu, wd, hs, hg, hu, ab, yb,
+    own_sem, x_sem, w_sem, d_sem, a_sem, y_sem, c_sem, ts_sem, tr_sem, xs_sem, xr_sem,
 ):
     groups = tabs.shape[0]
     tokens, width = x_hbm.shape
@@ -64,7 +64,7 @@
     xc = width // 2
     early = 2 * CAP
     late = groups * CAP - early
-    forward_at = steps // 2
+    forward_at = 5 * steps // 8
 
     me, core, partner, first_core = relatives()
 
@@ -134,6 +134,8 @@
     barrier = pltpu.get_barrier_semaphore()
     for d in range(1, groups):
         pl.semaphore_signal(barrier, inc=1, device_id={"ep": lax.rem(me + d, groups)}, device_id_type=MESH)
+    own_copy.wait()
+    route(xown[...], wr_ref[...], idx_ref, keep_ref, tab_ref)
     pl.semaphore_wait(barrier, groups - 1)
     for r in range(4):
         for k in range(2):
@@ -146,7 +148,6 @@
     for k in range(3):
         sends[k].start()
     tabs[core] = tab_ref[me]
-    own_copy.wait()
 
     def gated_pass(first, n_steps, n_rows, lhs, before, after):
         def activate(h):
@@ -248,6 +249,8 @@
                     arrived(4 + core)
                     sends[4].start()
                     sends[5].start()
+                    x_copy(2 + core, 0).start()
+                    x_copy(4 + core, 1).start()
 
         gated_pass(first, steps, n_rows, lambda it: xg[it // nt, :n_rows], before, after)
         a_copy(steps - 2, n_rows, base).wait()
@@ -267,9 +270,36 @@
     gather(1 - core, xbuf.at[0], (1 - core) * CAP)
     expert_pass(ns, early, 0)
 
+    n_slots = per_dev * CAP
+    lane = lax.broadcasted_iota(jnp.int32, (per_dev, n_slots), 1)
+    lead = lax.broadcasted_iota(jnp.int32, (per_dev, n_slots), 0) * CAP
+    inside = (lane >= lead) & (lane < lead + CAP)
+    spread = jnp.where(inside, 1.0, 0.0).astype(BF16)
+    want = jnp.sum(jnp.where(inside, lane - lead, 0).astype(F32), axis=0, keepdims=True)
+
+    def over_slots(v):
+        return lax.dot_general(v, spread, (((0,), (0,)), ((), ())), preferred_element_type=F32)
+
+    def c_copy(p):
+        return pltpu.make_async_copy(cbuf.at[lax.rem(p, 2)], comb_hbm.at[p], c_sem.at[lax.rem(p, 2)])
+
+    def build(p, _):
+        @pl.when(p >= 2)
+        def _():
+            c_copy(p - 2).wait()
+
+        hit = over_slots(tabs[p, :per_dev, :].astype(BF16)) == want
+        gate = tabs[p, per_dev:, :]
+        hi = gate.astype(BF16)
+        rest = gate - hi.astype(F32)
+        mid = rest.astype(BF16)
+        low = (rest - mid.astype(F32)).astype(BF16)
+        for k, piece in enumerate((hi, mid, low)):
+            cbuf[lax.rem(p, 2), k * tokens : (k + 1) * tokens] = jnp.where(hit, over_slots(piece), 0.0).astype(BF16)
+        c_copy(p).start()
+        return 0
+
     order = [2 + core, 4 + core, 3 - core, 5 - core, 6 + core, 7 - core]
-    x_copy(order[0], 0).start()
-    x_copy(order[1], 1).start()
     for n, pos in enumerate(order):
         x_copy(pos, n % 2).wait()
         gather(pos, xbuf.at[n % 2], (pos - 2) * CAP)
@@ -278,14 +308,19 @@
                 arrived(3 - core)
             if n + 2 == 3:
                 arrived(5 - core)
-            if n + 2 == 5:
-                arrived(7 - core)
-            if n + 2 == 4:
-                arrived(6 + core)
-                sends[6].start()
-            x_copy(order[n + 2], n % 2).start()
+            if n + 2 < 4:
+                x_copy(order[n + 2], n % 2).start()
+        if n == 3:
+            lax.fori_loop(0, groups, build, 0)
+            arrived(6 + core)
+            sends[6].start()
+            x_copy(order[4], 0).start()
+            arrived(7 - core)
+            x_copy(order[5], 1).start()
     expert_pass(ns + steps, late, early)
 
+    c_copy(groups - 2).wait()
+    c_copy(groups - 1).wait()
     for k in range(7):
         sends[k].wait_send()
     for r in range(4):
@@ -296,17 +331,14 @@
                     table_copy(r, k).wait_send()
             else:
                 table_copy(r, k).wait_send()
-    tabs_ref[...] = tabs[...]
 
 
 def down_kernel(
-    tab_ref, act_hbm, w2_hbm, ys_hbm, y_hbm,
+    comb_hbm, act_hbm, w2_hbm, ys_hbm, y_hbm,
     comb, act, part, wbuf, fsend, frecv, mine, bsend, brecv, acc, ybuf,
-    act_sem, w_sem, acc_sem, y_sem, fs_sem, fr_sem, bs_sem, br_sem, credit,
+    act_sem, w_sem, comb_sem, acc_sem, y_sem, fs_sem, fr_sem, bs_sem, br_sem, credit,
 ):
-    groups, pair, tokens = tab_ref.shape
-    per_dev = pair // 2
-    rows = per_dev * CAP
+    groups, per_dev, tokens = comb_hbm.shape[0], w2_hbm.shape[0], y_hbm.shape[0]
     cw = wbuf.shape[2]
     nc = acc.shape[0]
     steps = 4 * nc
@@ -322,13 +354,18 @@
     def act_copy(e):
         return pltpu.make_async_copy(act_hbm.at[e], act.at[e], act_sem.at[e])
 
+    def comb_copy(p):
+        return pltpu.make_async_copy(comb_hbm.at[p], comb.at[p], comb_sem.at[p])
+
     def acc_copy(c):
-        return pltpu.make_async_copy(ys_hbm.at[:, pl.ds(c * cw, cw)], acc.at[c], acc_sem.at[c])
+        return pltpu.make_async_copy(ys_hbm.at[:, pl.ds(pl.multiple_of(c * cw, cw), cw)], acc.at[c], acc_sem.at[c])
 
     for it in range(2):
         w_copy(it).start()
     for e in range(per_dev):
         act_copy(e).start()
+    for p in reversed(range(groups)):
+        comb_copy(p).start()
     for c in range(nc):
         acc_copy(c).start()
 
@@ -338,28 +375,6 @@
         pl.semaphore_signal(barrier, inc=1, device_id={"ep": first_core(3 - j) + core}, device_id_type=MESH)
     pl.semaphore_wait(barrier, 4)
 
-    lane = lax.broadcasted_iota(jnp.int32, (per_dev, rows), 1)
-    first = lax.broadcasted_iota(jnp.int32, (per_dev, rows), 0) * CAP
-    inside = (lane >= first) & (lane < first + CAP)
-    spread = jnp.where(inside, 1.0, 0.0).astype(BF16)
-    want = jnp.sum(jnp.where(inside, lane - first, 0).astype(F32), axis=0, keepdims=True)
-
-    def over_slots(v):
-        return lax.dot_general(v, spread, (((0,), (0,)), ((), ())), preferred_element_type=F32)
-
-    def build(s):
-        hit = over_slots(tab_ref[s, :per_dev, :].astype(BF16)) == want
-        gate = tab_ref[s, per_dev:, :]
-        hi = gate.astype(BF16)
-        rest = gate - hi.astype(F32)
-        mid = rest.astype(BF16)
-        low = (rest - mid.astype(F32)).astype(BF16)
-        for k, piece in enumerate((hi, mid, low)):
-            comb[s, k * tokens : (k + 1) * tokens] = jnp.where(hit, over_slots(piece), 0.0).astype(BF16)
-
-    for c in range(nc):
-        acc_copy(c).wait()
-
     def f_copy(slot):
         return pltpu.make_async_remote_copy(
             src_ref=fsend.at[slot], dst_ref=frecv.at[slot], send_sem=fs_sem.at[slot], recv_sem=fr_sem.at[slot],
@@ -396,6 +411,7 @@
 
         @pl.when(j == 3)
         def _():
+            acc_copy(c).wait()
             acc[c] = acc[c] + (mine[slot] + frecv[slot])
 
         @pl.when(h + 3 < steps)
@@ -434,8 +450,8 @@
 
             @pl.when(c == 0)
             def _():
-                build(p)
-                build(p + 1)
+                comb_copy(p).wait()
+                comb_copy(p + 1).wait()
 
             @pl.when(g >= 3)
             def _():
@@ -450,13 +466,13 @@
 
             f_copy(slot).start()
 
-            @pl.when(g >= 3)
-            def _():
-                launch(g - 3)
-
             @pl.when(g >= 2)
             def _():
-                consume(g - 2)
+                launch(g - 2)
+
+            @pl.when(g >= 1)
+            def _():
+                consume(g - 1)
 
             return 0
 
@@ -464,8 +480,6 @@
         return 0
 
     lax.fori_loop(0, nc, chunk, 0)
-    launch(steps - 3)
-    consume(steps - 2)
     launch(steps - 2)
     consume(steps - 1)
     for slot in range(3):
@@ -503,27 +517,23 @@
         rows = groups * CAP
         tn, cw = 256, 256
         nc = width // cw
-        tab = pl.pallas_call(
-            route_kernel,
-            out_shape=jax.ShapeDtypeStruct((groups, 2 * per_dev, tokens), F32),
-            in_specs=[vmem] * 4,
-            out_specs=vmem,
-            name="route",
-        )(hidden, w_router.T, top_idx.T, keep_mask.T)
         sff = shared_gate.shape[1]
         slots = 4
-        tabs, shared, act, _ = pl.pallas_call(
+        table = (groups, 2 * per_dev, tokens)
+        comb, shared, act, _ = pl.pallas_call(
             up_kernel,
             out_shape=(
-                jax.ShapeDtypeStruct(tab.shape, F32),
+                jax.ShapeDtypeStruct((groups, 3 * tokens, per_dev * CAP), BF16),
                 jax.ShapeDtypeStruct((tokens, width), F32),
                 jax.ShapeDtypeStruct((per_dev, rows, ff), BF16),
                 jax.ShapeDtypeStruct((groups, tokens, width), BF16),
             ),
-            in_specs=[vmem] + [hbm] * 6,
-            out_specs=(vmem, hbm, hbm, hbm),
+            in_specs=[vmem] * 3 + [hbm] * 6,
+            out_specs=(hbm,) * 4,
             scratch_shapes=[
-                pltpu.VMEM(tab.shape, F32),
+                pltpu.VMEM(table, F32),
+                pltpu.VMEM(table, F32),
+                pltpu.VMEM((2, 3 * tokens, per_dev * CAP), BF16),
                 pltpu.VMEM((tokens, width), BF16),
                 pltpu.VMEM((2, tokens, width), BF16),
                 pltpu.VMEM((per_dev, rows - 2 * CAP, width), BF16),
@@ -542,6 +552,7 @@
                 pltpu.SemaphoreType.DMA((3,)),
                 pltpu.SemaphoreType.DMA((2,)),
                 pltpu.SemaphoreType.DMA((2,)),
+                pltpu.SemaphoreType.DMA((2,)),
                 pltpu.SemaphoreType.DMA((groups,)),
                 pltpu.SemaphoreType.DMA((groups,)),
                 pltpu.SemaphoreType.DMA((7,)),
@@ -549,11 +560,11 @@
             ],
             compiler_params=pltpu.CompilerParams(vmem_limit_bytes=VMEM_BYTES, collective_id=1, has_side_effects=True),
             name="up",
-        )(tab, hidden, w_gate, w_up, shared_gate, shared_up, shared_down)
+        )(w_router.T, top_idx.T, keep_mask.T, hidden, w_gate, w_up, shared_gate, shared_up, shared_down)
         return pl.pallas_call(
             down_kernel,
             out_shape=jax.ShapeDtypeStruct((tokens, width), BF16),
-            in_specs=[vmem, hbm, hbm, hbm],
+            in_specs=[hbm] * 4,
             out_specs=hbm,
             scratch_shapes=[
                 pltpu.VMEM((groups, 3 * tokens, per_dev * CAP), BF16),
@@ -569,6 +580,7 @@
                 pltpu.VMEM((2, tokens, cw), BF16),
                 pltpu.SemaphoreType.DMA((per_dev,)),
                 pltpu.SemaphoreType.DMA((4,)),
+                pltpu.SemaphoreType.DMA((groups,)),
                 pltpu.SemaphoreType.DMA((nc,)),
                 pltpu.SemaphoreType.DMA((2,)),
                 pltpu.SemaphoreType.DMA((3,)),
@@ -580,6 +592,6 @@
             compiler_params=pltpu.CompilerParams(vmem_limit_bytes=VMEM_BYTES, collective_id=0, has_side_effects=True),
             cost_estimate=pl.CostEstimate(flops=8 * per_dev * rows * width * ff, bytes_accessed=2 * per_dev * width * ff, transcendentals=0),
             name="down",
-        )(tabs, act, w_down, shared)
+        )(comb, act, w_down, shared)
 
     return jax.shard_map(device_fn, mesh=mesh, in_specs=(tok_spec, P(), bank_spec, bank_spec, bank_spec, P(), P(), P(), tok_spec, tok_spec), out_specs=tok_spec, check_vma=False)

time: 351 us -> 352 us (level)
    pallas_call x2 -> x1, Pallas kernels: 195 us -> 198 us  [device_fn(): pl.pallas_call(up_kernel, out_shape=(jax.ShapeDtypeStruct((groups, 3 * to...]
where the time goes in v4:
time: 352 us
  Pallas kernels  348 us (99%)
    pallas_call x1, Pallas kernels, device_fn(): pl.pallas_call(up_kernel, out_shape=(jax.ShapeDtypeStruct((groups, 3 * to...  198 us
    pallas_call x1, Pallas kernels, device_fn(): pl.pallas_call(down_kernel, out_shape=jax.ShapeDtypeStruct((tokens, width...  150 us

profile of v4, /device:TPU:0, one launch (start us, length us, event | category | flops | bytes accessed | tf_op | source)
XLA Modules:
  0.0 351.8 jit_solution(1044499412330288072)
XLA Ops:
  0.0 198.0 %up.1 = (bf16[8,1536,768]{2,1,0:T(8,128)(2,1)}, f32[512,2560]{1,0:T(8,128)}, bf16[8,768,1536]{2,1,0:T(8,128)(2,1)}, bf16[8,512,2560]{2,1,0:T(8,128)(2,1)}) custom-call(bf16[64,2560]{1,0:T(8,128)(2,1)} %bitcast.3, s32[6,512]{1,0:T(8,128)} %bitcast.4, s32[6,512]{1,0:T(8,128)} %bitcast.5, bf16[512,2560]{1,0:T(8,128)(2,1)} %x_hbm.1, ...), custom_call_target="tpu_custom_call" | custom-call | tf_op jit(solution)/shard_map/up/pallas_call | solution.py:523
  198.0 150.4 %down.1 = bf16[512,2560]{1,0:T(8,128)(2,1)} custom-call(bf16[8,1536,768]{2,1,0:T(8,128)(2,1)} %get-tuple-element.8.comb_hbm, bf16[8,768,1536]{2,1,0:T(8,128)(2,1)} %get-tuple-element.9.act_hbm, bf16[8,1536,2560]{2,1,0:T(8,128)(2,1)} %w2_hbm.1, f32[512,2560]{1,0:T(8,128)} %get-tuple-element.10.ys_hbm), custom_call_target="tpu_custom_call" | custom-call | flops 193273528320 | bytes 62914560 | tf_op jit(solution)/shard_map/down/pallas_call | solution.py:564
  348.4 3.4 copy.12

commit v5 on v4

--- a/solution.py
+++ b/solution.py
@@ -51,20 +51,22 @@
 
 
 def up_kernel(
-    wr_ref, idx_ref, keep_ref, x_hbm, w1_hbm, w3_hbm, sg_hbm, su_hbm, sd_hbm, comb_hbm, ys_hbm, act_hbm, x_all,
-    tab_ref, tabs, cbuf, xown, xbuf, xg, dbuf, wg, wu, wd, hs, hg, hu, ab, yb,
-    own_sem, x_sem, w_sem, d_sem, a_sem, y_sem, c_sem, ts_sem, tr_sem, xs_sem, xr_sem,
+    wr_ref, idx_ref, keep_ref, x_hbm, w1_hbm, w3_hbm, sg_hbm, su_hbm, comb_hbm, hs_hbm, act_hbm, x_all,
+    tab_ref, tabs, cbuf, xown, xbuf, xg, dbuf, wg, wu, hs, hg, hu, ab,
+    own_sem, x_sem, w_sem, a_sem, hs_sem, c_sem, ts_sem, tr_sem, xs_sem, xr_sem,
 ):
     groups = tabs.shape[0]
     tokens, width = x_hbm.shape
     per_dev, _, ff = w1_hbm.shape
     slots, _, tn = wg.shape
-    nt, ns, nd = ff // tn, sg_hbm.shape[1] // tn, width // tn
+    nt, ns = ff // tn, sg_hbm.shape[1] // tn
     steps = per_dev * nt
     xc = width // 2
     early = 2 * CAP
     late = groups * CAP - early
-    forward_at = 5 * steps // 8
+    forward_at = 7 * steps // 8
+    near = late - 2 * CAP
+    ahead = 2 * nt
 
     me, core, partner, first_core = relatives()
 
@@ -104,11 +106,12 @@
             cols = pl.ds(pl.multiple_of(t * tn, tn), tn)
             go(sg_hbm.at[:, cols], su_hbm.at[:, cols])
 
-        @pl.when((t >= ns) & (t < ns + 2 * steps))
-        def _():
-            it = lax.rem(t - ns, steps)
-            cols = pl.ds(pl.multiple_of(lax.rem(it, nt) * tn, tn), tn)
-            go(w1_hbm.at[it // nt, :, cols], w3_hbm.at[it // nt, :, cols])
+        for begin, n_tiles in ((ns, steps), (ns + steps, ahead), (ns + steps + ahead, steps)):
+            @pl.when((t >= begin) & (t < begin + n_tiles))
+            def _():
+                it = t - begin
+                cols = pl.ds(pl.multiple_of(lax.rem(it, nt) * tn, tn), tn)
+                go(w1_hbm.at[it // nt, :, cols], w3_hbm.at[it // nt, :, cols])
 
     def w_wait(t):
         slot = lax.rem(t, slots)
@@ -116,20 +119,10 @@
         pltpu.make_async_copy(sg_hbm.at[:, pl.ds(0, tn)], wu.at[slot], w_sem.at[1, slot]).wait()
         return slot
 
-    def d_copy(n):
-        cols = pl.ds(pl.multiple_of(n * tn, tn), tn)
-        return pltpu.make_async_copy(sd_hbm.at[:, cols], wd.at[lax.rem(n, 3)], d_sem.at[lax.rem(n, 3)])
-
-    def y_copy(n):
-        cols = pl.ds(pl.multiple_of(n * tn, tn), tn)
-        return pltpu.make_async_copy(yb.at[lax.rem(n, 2)], ys_hbm.at[:, cols], y_sem.at[lax.rem(n, 2)])
-
     own_copy = pltpu.make_async_copy(x_hbm, xown, own_sem)
     own_copy.start()
     for t in range(slots - 1):
         w_start(t)
-    d_copy(0).start()
-    d_copy(1).start()
 
     barrier = pltpu.get_barrier_semaphore()
     for d in range(1, groups):
@@ -186,26 +179,8 @@
     hu[...] = jnp.zeros_like(hu)
     gated_pass(0, ns, tokens, lambda it: xown[...], lambda it: None, shared_after)
 
-    def shared_down(n, _):
-        slot = lax.rem(n, 2)
-
-        @pl.when(n + 2 < nd)
-        def _():
-            d_copy(n + 2).start()
-
-        d_copy(n).wait()
-
-        @pl.when(n >= 2)
-        def _():
-            y_copy(n - 2).wait()
-
-        yb[slot] = dot(hs[...], wd[lax.rem(n, 3)])
-        y_copy(n).start()
-        return 0
-
-    lax.fori_loop(0, nd, shared_down, 0)
-    y_copy(nd - 2).wait()
-    y_copy(nd - 1).wait()
+    hs_copy = pltpu.make_async_copy(hs, hs_hbm, hs_sem)
+    hs_copy.start()
 
     row = lax.broadcasted_iota(jnp.int32, (CAP, tokens), 0).astype(F32)
 
@@ -230,19 +205,19 @@
         slot = lax.rem(it, 2)
         return pltpu.make_async_copy(ab.at[slot, pl.ds(0, n_rows)], act_hbm.at[it // nt, pl.ds(base, n_rows), cols], a_sem.at[slot])
 
-    def expert_pass(first, n_rows, base):
-        def before(it):
-            @pl.when(it >= 2)
-            def _():
-                a_copy(it - 2, n_rows, base).wait()
-
-        def after(it):
-            @pl.when(it >= 0)
-            def _():
-                a_copy(it, n_rows, base).start()
+    def expert_pass(first, tile0, n_tiles, n_rows, row0, base):
+        def before(k):
+            @pl.when(k >= 2)
+            def _():
+                a_copy(tile0 + k - 2, n_rows, base).wait()
+
+        def after(k):
+            @pl.when(k >= 0)
+            def _():
+                a_copy(tile0 + k, n_rows, base).start()
 
             if base == 0:
-                @pl.when(it == forward_at)
+                @pl.when(k == forward_at)
                 def _():
                     arrived(2 + core)
                     sends[3].start()
@@ -252,9 +227,12 @@
                     x_copy(2 + core, 0).start()
                     x_copy(4 + core, 1).start()
 
-        gated_pass(first, steps, n_rows, lambda it: xg[it // nt, :n_rows], before, after)
-        a_copy(steps - 2, n_rows, base).wait()
-        a_copy(steps - 1, n_rows, base).wait()
+        def lhs(k):
+            return xg[(tile0 + k) // nt, row0 : row0 + n_rows]
+
+        gated_pass(first, n_tiles, n_rows, lhs, before, after)
+        a_copy(tile0 + n_tiles - 2, n_rows, base).wait()
+        a_copy(tile0 + n_tiles - 1, n_rows, base).wait()
 
     for p in range(groups):
         @pl.when(p != core)
@@ -268,7 +246,7 @@
     gather(core, xown, core * CAP)
     x_copy(1 - core, 0).wait()
     gather(1 - core, xbuf.at[0], (1 - core) * CAP)
-    expert_pass(ns, early, 0)
+    expert_pass(ns, 0, steps, early, 0, 0)
 
     n_slots = per_dev * CAP
     lane = lax.broadcasted_iota(jnp.int32, (per_dev, n_slots), 1)
@@ -312,13 +290,16 @@
                 x_copy(order[n + 2], n % 2).start()
         if n == 3:
             lax.fori_loop(0, groups, build, 0)
+            expert_pass(ns + steps, 0, ahead, near, 0, early)
             arrived(6 + core)
             sends[6].start()
             x_copy(order[4], 0).start()
             arrived(7 - core)
             x_copy(order[5], 1).start()
-    expert_pass(ns + steps, late, early)
-
+    expert_pass(ns + steps + ahead, 0, ahead, late - near, near, early + near)
+    expert_pass(ns + steps + 2 * ahead, ahead, steps - ahead, late, 0, early)
+
+    hs_copy.wait()
     c_copy(groups - 2).wait()
     c_copy(groups - 1).wait()
     for k in range(7):
@@ -334,9 +315,9 @@
 
 
 def down_kernel(
-    comb_hbm, act_hbm, w2_hbm, ys_hbm, y_hbm,
+    comb_hbm, act_hbm, w2_hbm, hs_hbm, sd_hbm, y_hbm, through,
     comb, act, part, wbuf, fsend, frecv, mine, bsend, brecv, acc, ybuf,
-    act_sem, w_sem, comb_sem, acc_sem, y_sem, fs_sem, fr_sem, bs_sem, br_sem, credit,
+    act_sem, w_sem, comb_sem, hs_sem, y_sem, fs_sem, fr_sem, bs_sem, br_sem, ts_sem, tr_sem, credit,
 ):
     groups, per_dev, tokens = comb_hbm.shape[0], w2_hbm.shape[0], y_hbm.shape[0]
     cw = wbuf.shape[2]
@@ -357,8 +338,15 @@
     def comb_copy(p):
         return pltpu.make_async_copy(comb_hbm.at[p], comb.at[p], comb_sem.at[p])
 
-    def acc_copy(c):
-        return pltpu.make_async_copy(ys_hbm.at[:, pl.ds(pl.multiple_of(c * cw, cw), cw)], acc.at[c], acc_sem.at[c])
+    ff = act.shape[2]
+
+    def hs_copy(h):
+        return pltpu.make_async_copy(hs_hbm.at[:, pl.ds(h * ff, ff)], act.at[h, pl.ds(0, tokens)], hs_sem.at[h])
+
+    def sd_copy(c, h):
+        cols = pl.ds(pl.multiple_of(c * cw, cw), cw)
+        slot = 2 * lax.rem(c, 2) + h
+        return pltpu.make_async_copy(sd_hbm.at[pl.ds(h * ff, ff), cols], wbuf.at[slot], w_sem.at[slot])
 
     for it in range(2):
         w_copy(it).start()
@@ -366,8 +354,6 @@
         act_copy(e).start()
     for p in reversed(range(groups)):
         comb_copy(p).start()
-    for c in range(nc):
-        acc_copy(c).start()
 
     barrier = pltpu.get_barrier_semaphore()
     pl.semaphore_signal(barrier, inc=1, device_id={"ep": partner}, device_id_type=MESH)
@@ -386,6 +372,26 @@
             src_ref=bsend.at[j, slot], dst_ref=brecv.at[j, c], send_sem=bs_sem.at[j, slot], recv_sem=br_sem.at[j, c],
             device_id={"ep": first_core(3 - j) + core}, device_id_type=MESH)
 
+    def t_copy(c):
+        slot = lax.rem(c, 2)
+        return pltpu.make_async_remote_copy(
+            src_ref=bsend.at[0, slot], dst_ref=through.at[c], send_sem=bs_sem.at[0, slot], recv_sem=tr_sem.at[c],
+            device_id={"ep": first_core(1 + core) + core}, device_id_type=MESH)
+
+    def pass_on(c):
+        slot = lax.rem(c, 2)
+        return pltpu.make_async_remote_copy(
+            src_ref=through.at[c], dst_ref=brecv.at[0, c], send_sem=ts_sem.at[slot], recv_sem=br_sem.at[0, c],
+            device_id={"ep": first_core(2 - core) + core}, device_id_type=MESH)
+
+    def relay(c):
+        @pl.when(c >= 2)
+        def _():
+            pass_on(c - 2).wait_send()
+
+        t_copy(c).wait_recv()
+        pass_on(c).start()
+
     def combine(s):
         pieces = dot(comb[s], part[s])
         return pieces[:tokens] + pieces[tokens : 2 * tokens] + pieces[2 * tokens :]
@@ -393,7 +399,11 @@
     def launch(h):
         j = lax.rem(h, 4)
 
-        @pl.when(j < 3)
+        @pl.when(j == 0)
+        def _():
+            t_copy(h // 4).start()
+
+        @pl.when((j > 0) & (j < 3))
         def _():
             b_copy(j, h // 4).start()
 
@@ -411,8 +421,7 @@
 
         @pl.when(j == 3)
         def _():
-            acc_copy(c).wait()
-            acc[c] = acc[c] + (mine[slot] + frecv[slot])
+            acc[c] = mine[slot] + frecv[slot]
 
         @pl.when(h + 3 < steps)
         def _():
@@ -476,7 +485,19 @@
 
             return 0
 
+        @pl.when(c == nc - 1)
+        def _():
+            for h in range(2):
+                hs_copy(h).start()
+                sd_copy(0, h).start()
+                sd_copy(1, h).start()
+
         lax.fori_loop(0, 4, pair_step, 0)
+
+        @pl.when(c >= 1)
+        def _():
+            relay(c - 1)
+
         return 0
 
     lax.fori_loop(0, nc, chunk, 0)
@@ -486,22 +507,54 @@
         f_copy(slot).wait_send()
 
     def y_copy(c):
-        return pltpu.make_async_copy(ybuf.at[c % 2], y_hbm.at[:, pl.ds(c * cw, cw)], y_sem.at[c % 2])
-
-    for c in range(nc):
+        cols = pl.ds(pl.multiple_of(c * cw, cw), cw)
+        return pltpu.make_async_copy(ybuf.at[lax.rem(c, 2)], y_hbm.at[:, cols], y_sem.at[lax.rem(c, 2)])
+
+    for h in range(2):
+        hs_copy(h).wait()
+
+    def finish(c, _):
+        for h in range(2):
+            sd_copy(c, h).wait()
+        slot = 2 * lax.rem(c, 2)
+        shared = dot(act[0, :tokens], wbuf[slot]) + dot(act[1, :tokens], wbuf[slot + 1])
+
+        @pl.when(c + 2 < nc)
+        def _():
+            for h in range(2):
+                sd_copy(c + 2, h).start()
+
+        acc[c] = acc[c] + shared
+
+        @pl.when(c == nc // 2)
+        def _():
+            relay(nc - 1)
+
+        return 0
+
+    lax.fori_loop(0, nc, finish, 0)
+
+    def write(c, _):
         for j in range(3):
             b_copy(j, c).wait_recv()
-            if c >= nc - 2:
-                b_copy(j, c).wait_send()
-        if c >= 2:
+
+        @pl.when(c >= 2)
+        def _():
             y_copy(c - 2).wait()
+
         total = acc[c]
         for j in range(3):
             total = total + brecv[j, c].astype(F32)
-        ybuf[c % 2] = total.astype(BF16)
+        ybuf[lax.rem(c, 2)] = total.astype(BF16)
         y_copy(c).start()
-    y_copy(nc - 2).wait()
-    y_copy(nc - 1).wait()
+        return 0
+
+    lax.fori_loop(0, nc, write, 0)
+    for c in (nc - 2, nc - 1):
+        y_copy(c).wait()
+        pass_on(c).wait_send()
+        for j in range(3):
+            b_copy(j, c).wait_send()
 
 
 def solution(mesh):
@@ -520,15 +573,15 @@
         sff = shared_gate.shape[1]
         slots = 4
         table = (groups, 2 * per_dev, tokens)
-        comb, shared, act, _ = pl.pallas_call(
+        comb, shared_act, act, _ = pl.pallas_call(
             up_kernel,
             out_shape=(
                 jax.ShapeDtypeStruct((groups, 3 * tokens, per_dev * CAP), BF16),
-                jax.ShapeDtypeStruct((tokens, width), F32),
+                jax.ShapeDtypeStruct((tokens, sff), BF16),
                 jax.ShapeDtypeStruct((per_dev, rows, ff), BF16),
                 jax.ShapeDtypeStruct((groups, tokens, width), BF16),
             ),
-            in_specs=[vmem] * 3 + [hbm] * 6,
+            in_specs=[vmem] * 3 + [hbm] * 5,
             out_specs=(hbm,) * 4,
             scratch_shapes=[
                 pltpu.VMEM(table, F32),
@@ -540,18 +593,15 @@
                 pltpu.VMEM((per_dev * CAP, tokens), BF16),
                 pltpu.VMEM((slots, width, tn), BF16),
                 pltpu.VMEM((slots, width, tn), BF16),
-                pltpu.VMEM((3, sff, tn), BF16),
                 pltpu.VMEM((tokens, sff), BF16),
                 pltpu.VMEM((2, rows - 2 * CAP, tn), F32),
                 pltpu.VMEM((2, rows - 2 * CAP, tn), F32),
                 pltpu.VMEM((2, rows - 2 * CAP, tn), BF16),
-                pltpu.VMEM((2, tokens, tn), F32),
                 pltpu.SemaphoreType.DMA,
                 pltpu.SemaphoreType.DMA((2,)),
                 pltpu.SemaphoreType.DMA((2, slots)),
-                pltpu.SemaphoreType.DMA((3,)),
                 pltpu.SemaphoreType.DMA((2,)),
-                pltpu.SemaphoreType.DMA((2,)),
+                pltpu.SemaphoreType.DMA,
                 pltpu.SemaphoreType.DMA((2,)),
                 pltpu.SemaphoreType.DMA((groups,)),
                 pltpu.SemaphoreType.DMA((groups,)),
@@ -560,12 +610,15 @@
             ],
             compiler_params=pltpu.CompilerParams(vmem_limit_bytes=VMEM_BYTES, collective_id=1, has_side_effects=True),
             name="up",
-        )(w_router.T, top_idx.T, keep_mask.T, hidden, w_gate, w_up, shared_gate, shared_up, shared_down)
-        return pl.pallas_call(
+        )(w_router.T, top_idx.T, keep_mask.T, hidden, w_gate, w_up, shared_gate, shared_up)
+        y, _ = pl.pallas_call(
             down_kernel,
-            out_shape=jax.ShapeDtypeStruct((tokens, width), BF16),
-            in_specs=[hbm] * 4,
-            out_specs=hbm,
+            out_shape=(
+                jax.ShapeDtypeStruct((tokens, width), BF16),
+                jax.ShapeDtypeStruct((nc, tokens, cw), BF16),
+            ),
+            in_specs=[hbm] * 5,
+            out_specs=(hbm, hbm),
             scratch_shapes=[
                 pltpu.VMEM((groups, 3 * tokens, per_dev * CAP), BF16),
                 pltpu.VMEM((per_dev, rows, ff), BF16),
@@ -581,17 +634,20 @@
                 pltpu.SemaphoreType.DMA((per_dev,)),
                 pltpu.SemaphoreType.DMA((4,)),
                 pltpu.SemaphoreType.DMA((groups,)),
-                pltpu.SemaphoreType.DMA((nc,)),
+                pltpu.SemaphoreType.DMA((2,)),
                 pltpu.SemaphoreType.DMA((2,)),
                 pltpu.SemaphoreType.DMA((3,)),
                 pltpu.SemaphoreType.DMA((3,)),
                 pltpu.SemaphoreType.DMA((3, 2)),
                 pltpu.SemaphoreType.DMA((3, nc)),
+                pltpu.SemaphoreType.DMA((2,)),
+                pltpu.SemaphoreType.DMA((nc,)),
                 pltpu.SemaphoreType.REGULAR,
             ],
             compiler_params=pltpu.CompilerParams(vmem_limit_bytes=VMEM_BYTES, collective_id=0, has_side_effects=True),
             cost_estimate=pl.CostEstimate(flops=8 * per_dev * rows * width * ff, bytes_accessed=2 * per_dev * width * ff, transcendentals=0),
             name="down",
-        )(comb, act, w_down, shared)
+        )(comb, act, w_down, shared_act, shared_down)
+        return y
 
     return jax.shard_map(device_fn, mesh=mesh, in_specs=(tok_spec, P(), bank_spec, bank_spec, bank_spec, P(), P(), P(), tok_spec, tok_spec), out_specs=tok_spec, check_vma=False)

time: 352 us -> 347 us (0.986)
  Pallas kernels: 348 us -> 343 us
    pallas_call x1, Pallas kernels: 198 us -> 192 us  [device_fn(): pl.pallas_call(up_kernel, out_shape=(jax.ShapeDtypeStruct((groups, 3 * to...]
where the time goes in v5:
time: 347 us
  Pallas kernels  343 us (99%)
    pallas_call x1, Pallas kernels, device_fn(): pl.pallas_call(up_kernel, out_shape=(jax.ShapeDtypeStruct((groups, 3 * to...  192 us
    pallas_call x1, Pallas kernels, device_fn(): pl.pallas_call(down_kernel, out_shape=(jax.ShapeDtypeStruct((tokens, widt...  151 us

profile of v5, /device:TPU:0, one launch (start us, length us, event | category | flops | bytes accessed | tf_op | source)
XLA Modules:
  0.0 346.9 jit_solution(3804772211470291650)
XLA Ops:
  0.0 192.1 %up.1 = (bf16[8,1536,768]{2,1,0:T(8,128)(2,1)}, bf16[512,3072]{1,0:T(8,128)(2,1)}, bf16[8,768,1536]{2,1,0:T(8,128)(2,1)}, bf16[8,512,2560]{2,1,0:T(8,128)(2,1)}) custom-call(bf16[64,2560]{1,0:T(8,128)(2,1)} %bitcast.3, s32[6,512]{1,0:T(8,128)} %bitcast.4, s32[6,512]{1,0:T(8,128)} %bitcast.5, bf16[512,2560]{1,0:T(8,128)(2,1)} %x_hbm.1, ...), custom_call_target="tpu_custom_call" | custom-call | tf_op jit(solution)/shard_map/up/pallas_call | solution.py:576
  192.1 151.4 %down.1 = (bf16[512,2560]{1,0:T(8,128)(2,1)}, bf16[10,512,256]{2,1,0:T(8,128)(2,1)}) custom-call(bf16[8,1536,768]{2,1,0:T(8,128)(2,1)} %get-tuple-element.9.comb_hbm, bf16[8,768,1536]{2,1,0:T(8,128)(2,1)} %get-tuple-element.10.act_hbm, bf16[8,1536,2560]{2,1,0:T(8,128)(2,1)} %w2_hbm.1, bf16[512,3072]{1,0:T(8,128)(2,1)} %get-tuple-element.11.hs_hbm, ...), custom_call_target="tpu_custom_call" | custom-call | flops 193273528320 | bytes 62914560 | tf_op jit(solution)/shard_map/down/pallas_call | solution.py:614
  343.5 3.4 copy.12

commit v6 on v5

--- a/solution.py
+++ b/solution.py
@@ -361,9 +361,10 @@
         pl.semaphore_signal(barrier, inc=1, device_id={"ep": first_core(3 - j) + core}, device_id_type=MESH)
     pl.semaphore_wait(barrier, 4)
 
-    def f_copy(slot):
+    def f_copy(g):
+        out, land = lax.rem(g, 3), lax.rem(g, 4)
         return pltpu.make_async_remote_copy(
-            src_ref=fsend.at[slot], dst_ref=frecv.at[slot], send_sem=fs_sem.at[slot], recv_sem=fr_sem.at[slot],
+            src_ref=fsend.at[out], dst_ref=frecv.at[land], send_sem=fs_sem.at[out], recv_sem=fr_sem.at[land],
             device_id={"ep": partner}, device_id_type=MESH)
 
     def b_copy(j, c):
@@ -396,38 +397,32 @@
         pieces = dot(comb[s], part[s])
         return pieces[:tokens] + pieces[tokens : 2 * tokens] + pieces[2 * tokens :]
 
-    def launch(h):
-        j = lax.rem(h, 4)
-
-        @pl.when(j == 0)
-        def _():
-            t_copy(h // 4).start()
-
-        @pl.when((j > 0) & (j < 3))
-        def _():
-            b_copy(j, h // 4).start()
-
-    def consume(h):
-        slot, c, j = lax.rem(h, 3), h // 4, lax.rem(h, 4)
-        f_copy(slot).wait_recv()
-
-        @pl.when(j < 3)
-        def _():
+    def launch(j, c):
+        if j == 0:
+            t_copy(c).start()
+        elif j < 3:
+            b_copy(j, c).start()
+
+    def settle_wait(j, c):
+        f_copy(4 * c + j).wait_recv()
+        if j < 3:
             @pl.when(c >= 2)
             def _():
                 b_copy(j, c - 2).wait_send()
 
-            bsend[j, lax.rem(c, 2)] = (mine[slot] + frecv[slot]).astype(BF16)
-
-        @pl.when(j == 3)
-        def _():
-            acc[c] = mine[slot] + frecv[slot]
-
-        @pl.when(h + 3 < steps)
+    def settle(j, c):
+        total = mine[lax.rem(4 * c + j, 3)] + frecv[j]
+        if j < 3:
+            bsend[j, lax.rem(c, 2)] = total.astype(BF16)
+        else:
+            acc[c] = total
+
+    def credit_back(h):
+        @pl.when((h >= 0) & (h + 4 < steps))
         def _():
             pl.semaphore_signal(credit, inc=1, device_id={"ep": partner}, device_id_type=MESH)
 
-    def chunk(c, _):
+    def chunk(c, _, first=False):
         def down(i, _):
             for h in range(2):
                 it = c * per_dev + 2 * i + h
@@ -452,39 +447,6 @@
 
         lax.fori_loop(0, per_dev // 2, down, 0)
 
-        def pair_step(j, _):
-            g = 4 * c + j
-            slot = lax.rem(g, 3)
-            p = 2 * (3 - j)
-
-            @pl.when(c == 0)
-            def _():
-                comb_copy(p).wait()
-                comb_copy(p + 1).wait()
-
-            @pl.when(g >= 3)
-            def _():
-                f_copy(slot).wait_send()
-
-            fsend[slot] = combine(p + 1 - core)
-            mine[slot] = combine(p + core)
-
-            @pl.when(g >= 3)
-            def _():
-                pl.semaphore_wait(credit, 1)
-
-            f_copy(slot).start()
-
-            @pl.when(g >= 2)
-            def _():
-                launch(g - 2)
-
-            @pl.when(g >= 1)
-            def _():
-                consume(g - 1)
-
-            return 0
-
         @pl.when(c == nc - 1)
         def _():
             for h in range(2):
@@ -492,7 +454,36 @@
                 sd_copy(0, h).start()
                 sd_copy(1, h).start()
 
-        lax.fori_loop(0, 4, pair_step, 0)
+        for j in range(4):
+            g = 4 * c + j
+            p = 2 * (3 - j)
+            jj, cc = (j + 1) % 4, c if j == 3 else c - 1
+
+            @pl.when(c == 0)
+            def _():
+                comb_copy(p).wait()
+                comb_copy(p + 1).wait()
+
+            @pl.when(g >= 3)
+            def _():
+                f_copy(g - 3).wait_send()
+                settle_wait(jj, cc)
+
+            if not first or j == 3:
+                settle(jj, cc)
+            fsend[lax.rem(g, 3)] = combine(p + 1 - core)
+            mine[lax.rem(g, 3)] = combine(p + core)
+            credit_back(g - 3)
+
+            @pl.when(g >= 4)
+            def _():
+                pl.semaphore_wait(credit, 1)
+
+            f_copy(g).start()
+
+            @pl.when(g >= 3)
+            def _():
+                launch(jj, cc)
 
         @pl.when(c >= 1)
         def _():
@@ -500,11 +491,14 @@
 
         return 0
 
-    lax.fori_loop(0, nc, chunk, 0)
-    launch(steps - 2)
-    consume(steps - 1)
-    for slot in range(3):
-        f_copy(slot).wait_send()
+    chunk(0, 0, first=True)
+    lax.fori_loop(1, nc, chunk, 0)
+    for j in range(1, 4):
+        settle_wait(j, nc - 1)
+        settle(j, nc - 1)
+        launch(j, nc - 1)
+    for g in range(steps - 3, steps):
+        f_copy(g).wait_send()
 
     def y_copy(c):
         cols = pl.ds(pl.multiple_of(c * cw, cw), cw)
@@ -516,25 +510,6 @@
     def finish(c, _):
         for h in range(2):
             sd_copy(c, h).wait()
-        slot = 2 * lax.rem(c, 2)
-        shared = dot(act[0, :tokens], wbuf[slot]) + dot(act[1, :tokens], wbuf[slot + 1])
-
-        @pl.when(c + 2 < nc)
-        def _():
-            for h in range(2):
-                sd_copy(c + 2, h).start()
-
-        acc[c] = acc[c] + shared
-
-        @pl.when(c == nc // 2)
-        def _():
-            relay(nc - 1)
-
-        return 0
-
-    lax.fori_loop(0, nc, finish, 0)
-
-    def write(c, _):
         for j in range(3):
             b_copy(j, c).wait_recv()
 
@@ -542,14 +517,25 @@
         def _():
             y_copy(c - 2).wait()
 
-        total = acc[c]
+        slot = 2 * lax.rem(c, 2)
+        total = acc[c] + dot(act[0, :tokens], wbuf[slot]) + dot(act[1, :tokens], wbuf[slot + 1])
         for j in range(3):
             total = total + brecv[j, c].astype(F32)
         ybuf[lax.rem(c, 2)] = total.astype(BF16)
         y_copy(c).start()
+
+        @pl.when(c + 2 < nc)
+        def _():
+            for h in range(2):
+                sd_copy(c + 2, h).start()
+
+        @pl.when(c == nc // 2)
+        def _():
+            relay(nc - 1)
+
         return 0
 
-    lax.fori_loop(0, nc, write, 0)
+    lax.fori_loop(0, nc, finish, 0)
     for c in (nc - 2, nc - 1):
         y_copy(c).wait()
         pass_on(c).wait_send()
@@ -625,7 +611,7 @@
                 pltpu.VMEM((groups, per_dev * CAP, cw), BF16),
                 pltpu.VMEM((4, ff, cw), BF16),
                 pltpu.VMEM((3, tokens, cw), F32),
-                pltpu.VMEM((3, tokens, cw), F32),
+                pltpu.VMEM((4, tokens, cw), F32),
                 pltpu.VMEM((3, tokens, cw), F32),
                 pltpu.VMEM((3, 2, tokens, cw), BF16),
                 pltpu.VMEM((3, nc, tokens, cw), BF16),
@@ -637,7 +623,7 @@
                 pltpu.SemaphoreType.DMA((2,)),
                 pltpu.SemaphoreType.DMA((2,)),
                 pltpu.SemaphoreType.DMA((3,)),
-                pltpu.SemaphoreType.DMA((3,)),
+                pltpu.SemaphoreType.DMA((4,)),
                 pltpu.SemaphoreType.DMA((3, 2)),
                 pltpu.SemaphoreType.DMA((3, nc)),
                 pltpu.SemaphoreType.DMA((2,)),

time: 347 us -> 345 us (level)
  no operation moved by 1% of the time
where the time goes in v6:
time: 345 us; the launch traced here: 344 us
  Pallas kernels  341 us (99%)
    pallas_call x1, Pallas kernels, device_fn(): pl.pallas_call(up_kernel, out_shape=(jax.ShapeDtypeStruct((groups, 3 * to...  192 us
    pallas_call x1, Pallas kernels, device_fn(): pl.pallas_call(down_kernel, out_shape=(jax.ShapeDtypeStruct((tokens, widt...  149 us

profile of v6, /device:TPU:0, one launch (start us, length us, event | category | flops | bytes accessed | tf_op | source)
XLA Modules:
  0.0 344.3 jit_solution(131424792676814704)
XLA Ops:
  0.0 192.1 %up.1 = (bf16[8,1536,768]{2,1,0:T(8,128)(2,1)}, bf16[512,3072]{1,0:T(8,128)(2,1)}, bf16[8,768,1536]{2,1,0:T(8,128)(2,1)}, bf16[8,512,2560]{2,1,0:T(8,128)(2,1)}) custom-call(bf16[64,2560]{1,0:T(8,128)(2,1)} %bitcast.3, s32[6,512]{1,0:T(8,128)} %bitcast.4, s32[6,512]{1,0:T(8,128)} %bitcast.5, bf16[512,2560]{1,0:T(8,128)(2,1)} %x_hbm.1, ...), custom_call_target="tpu_custom_call" | custom-call | tf_op jit(solution)/shard_map/up/pallas_call | solution.py:562
  192.1 148.8 %down.1 = (bf16[512,2560]{1,0:T(8,128)(2,1)}, bf16[10,512,256]{2,1,0:T(8,128)(2,1)}) custom-call(bf16[8,1536,768]{2,1,0:T(8,128)(2,1)} %get-tuple-element.9.comb_hbm, bf16[8,768,1536]{2,1,0:T(8,128)(2,1)} %get-tuple-element.10.act_hbm, bf16[8,1536,2560]{2,1,0:T(8,128)(2,1)} %w2_hbm.1, bf16[512,3072]{1,0:T(8,128)(2,1)} %get-tuple-element.11.hs_hbm, ...), custom_call_target="tpu_custom_call" | custom-call | flops 193273528320 | bytes 62914560 | tf_op jit(solution)/shard_map/down/pallas_call | solution.py:600
  340.9 3.4 copy.12

commit v7 on v6

--- a/solution.py
+++ b/solution.py
@@ -67,6 +67,7 @@
     forward_at = 7 * steps // 8
     near = late - 2 * CAP
     ahead = 2 * nt
+    hand_at = 7 * ahead // 12
 
     me, core, partner, first_core = relatives()
 
@@ -216,6 +217,13 @@
             def _():
                 a_copy(tile0 + k, n_rows, base).start()
 
+            if n_rows == near:
+                @pl.when(k == hand_at)
+                def _():
+                    arrived(6 + core)
+                    sends[6].start()
+                    x_copy(6 + core, 0).start()
+
             if base == 0:
                 @pl.when(k == forward_at)
                 def _():
@@ -291,9 +299,6 @@
         if n == 3:
             lax.fori_loop(0, groups, build, 0)
             expert_pass(ns + steps, 0, ahead, near, 0, early)
-            arrived(6 + core)
-            sends[6].start()
-            x_copy(order[4], 0).start()
             arrived(7 - core)
             x_copy(order[5], 1).start()
     expert_pass(ns + steps + ahead, 0, ahead, late - near, near, early + near)
@@ -350,10 +355,8 @@
 
     for it in range(2):
         w_copy(it).start()
-    for e in range(per_dev):
+    for e in range(4):
         act_copy(e).start()
-    for p in reversed(range(groups)):
-        comb_copy(p).start()
 
     barrier = pltpu.get_barrier_semaphore()
     pl.semaphore_signal(barrier, inc=1, device_id={"ep": partner}, device_id_type=MESH)
@@ -399,7 +402,13 @@
 
     def launch(j, c):
         if j == 0:
-            t_copy(c).start()
+            @pl.when(c < nc - 1)
+            def _():
+                t_copy(c).start()
+
+            @pl.when(c == nc - 1)
+            def _():
+                b_copy(0, c).start()
         elif j < 3:
             b_copy(j, c).start()
 
@@ -422,7 +431,7 @@
         def _():
             pl.semaphore_signal(credit, inc=1, device_id={"ep": partner}, device_id_type=MESH)
 
-    def chunk(c, _, first=False):
+    def chunk(c, _, early=None):
         def down(i, _):
             for h in range(2):
                 it = c * per_dev + 2 * i + h
@@ -431,9 +440,20 @@
                 def _():
                     w_copy(it + 2).start()
 
-                @pl.when(c == 0)
-                def _():
+                if early == 0:
                     act_copy(2 * i + h).wait()
+
+                    @pl.when(2 * i + h + 4 < per_dev)
+                    def _():
+                        act_copy(2 * i + h + 4).start()
+
+                    @pl.when(i == per_dev // 2 - 2)
+                    def _():
+                        comb_copy(6 + h).start()
+
+                    @pl.when(i == per_dev // 2 - 1)
+                    def _():
+                        comb_copy(4 + h).start()
 
             for h in range(2):
                 w_copy(c * per_dev + 2 * i + h).wait()
@@ -459,21 +479,26 @@
             p = 2 * (3 - j)
             jj, cc = (j + 1) % 4, c if j == 3 else c - 1
 
-            @pl.when(c == 0)
-            def _():
-                comb_copy(p).wait()
-                comb_copy(p + 1).wait()
+            if early == 0:
+                for k in range(2):
+                    comb_copy(p + k).wait()
+                    if j < 2:
+                        comb_copy(p - 4 + k).start()
+
+            late = early is None or (early == 1 and j >= 2)
 
             @pl.when(g >= 3)
             def _():
                 f_copy(g - 3).wait_send()
-                settle_wait(jj, cc)
-
-            if not first or j == 3:
+                if late:
+                    settle_wait(jj, cc)
+
+            if late:
                 settle(jj, cc)
             fsend[lax.rem(g, 3)] = combine(p + 1 - core)
             mine[lax.rem(g, 3)] = combine(p + core)
-            credit_back(g - 3)
+            if late:
+                credit_back(g - 3)
 
             @pl.when(g >= 4)
             def _():
@@ -481,9 +506,13 @@
 
             f_copy(g).start()
 
-            @pl.when(g >= 3)
-            def _():
+            if late:
                 launch(jj, cc)
+            elif early == 0 and j >= 1:
+                settle_wait(j - 1, 0)
+                settle(j - 1, 0)
+                credit_back(j - 1)
+                launch(j - 1, 0)
 
         @pl.when(c >= 1)
         def _():
@@ -491,8 +520,9 @@
 
         return 0
 
-    chunk(0, 0, first=True)
-    lax.fori_loop(1, nc, chunk, 0)
+    for c in range(2):
+        chunk(c, 0, early=c)
+    lax.fori_loop(2, nc, chunk, 0)
     for j in range(1, 4):
         settle_wait(j, nc - 1)
         settle(j, nc - 1)
@@ -529,16 +559,12 @@
             for h in range(2):
                 sd_copy(c + 2, h).start()
 
-        @pl.when(c == nc // 2)
-        def _():
-            relay(nc - 1)
-
         return 0
 
     lax.fori_loop(0, nc, finish, 0)
     for c in (nc - 2, nc - 1):
         y_copy(c).wait()
-        pass_on(c).wait_send()
+        pass_on(c - 1).wait_send()
         for j in range(3):
             b_copy(j, c).wait_send()
 

time: 345 us -> 335 us (0.971)
  Pallas kernels: 341 us -> 330 us
    pallas_call x1, Pallas kernels: 149 us -> 142 us  [device_fn(): pl.pallas_call(down_kernel, out_shape=(jax.ShapeDtypeStruct((tokens, widt...]
    pallas_call x1, Pallas kernels: 192 us -> 189 us  [device_fn(): pl.pallas_call(up_kernel, out_shape=(jax.ShapeDtypeStruct((groups, 3 * to...]
where the time goes in v7:
time: 335 us; the launch traced here: 334 us
  Pallas kernels  330 us (99%)
  local copies, waits for them, and re-layouts  3.4 us (1%)
    pallas_call x1, Pallas kernels, device_fn(): pl.pallas_call(up_kernel, out_shape=(jax.ShapeDtypeStruct((groups, 3 * to...  189 us
    pallas_call x1, Pallas kernels, device_fn(): pl.pallas_call(down_kernel, out_shape=(jax.ShapeDtypeStruct((tokens, widt...  142 us

profile of v7, /device:TPU:0, one launch (start us, length us, event | category | flops | bytes accessed | tf_op | source)
XLA Modules:
  0.0 333.6 jit_solution(15717561165605711232)
XLA Ops:
  0.0 188.5 %up.1 = (bf16[8,1536,768]{2,1,0:T(8,128)(2,1)}, bf16[512,3072]{1,0:T(8,128)(2,1)}, bf16[8,768,1536]{2,1,0:T(8,128)(2,1)}, bf16[8,512,2560]{2,1,0:T(8,128)(2,1)}) custom-call(bf16[64,2560]{1,0:T(8,128)(2,1)} %bitcast.3, s32[6,512]{1,0:T(8,128)} %bitcast.4, s32[6,512]{1,0:T(8,128)} %bitcast.5, bf16[512,2560]{1,0:T(8,128)(2,1)} %x_hbm.1, ...), custom_call_target="tpu_custom_call" | custom-call | tf_op jit(solution)/shard_map/up/pallas_call | solution.py:588
  188.5 141.6 %down.1 = (bf16[512,2560]{1,0:T(8,128)(2,1)}, bf16[10,512,256]{2,1,0:T(8,128)(2,1)}) custom-call(bf16[8,1536,768]{2,1,0:T(8,128)(2,1)} %get-tuple-element.9.comb_hbm, bf16[8,768,1536]{2,1,0:T(8,128)(2,1)} %get-tuple-element.10.act_hbm, bf16[8,1536,2560]{2,1,0:T(8,128)(2,1)} %w2_hbm.1, bf16[512,3072]{1,0:T(8,128)(2,1)} %get-tuple-element.11.hs_hbm, ...), custom_call_target="tpu_custom_call" | custom-call | flops 193273528320 | bytes 62914560 | tf_op jit(solution)/shard_map/down/pallas_call | solution.py:626
  330.2 3.4 %copy.12 = bf16[512,2560]{1,0:T(8,128)(2,1)} copy(bf16[512,2560]{1,0:T(8,128)(2,1)} %get-tuple-element.12) | data formatting | bytes 5242880
